TPU v7x, 32 devices: a whole 2x2x4 slice. The times are simulated.
32 devices in a mesh: fsdp: 4 (over z), ctx: 4 (over y, x), tp: 2 (over core).
Axes of the slice: x: 2, y: 2, z: 4, core: 2. Of those that a mesh axis runs over, the one named last changes fastest.
Arguments:
- block_input: bfloat16 [4, 1024, 1600], P('fsdp', 'ctx'), may hold values from -8 to 8
- segments: int32 [4, 1024], P('fsdp', 'ctx'), may hold values from 0 to 3, never falling along the last dimension, each value on 1 to 512 neighbouring positions
- ln1_gain: float32 [1600], replicated, may hold values from 0.5 to 1.5
- ln1_shift: float32 [1600], replicated, may hold values from -3 to 3
- qkv_weight: bfloat16 [1600, 4800], P('fsdp'), may hold values from -4 to 4
- out_weight: bfloat16 [1600, 1600], P(None, 'fsdp'), may hold values from -0.4375 to 0.4375
- ln2_gain: float32 [1600], replicated, may hold values from 0.5 to 1.5
- ln2_shift: float32 [1600], replicated, may hold values from -3 to 3
- fc_weight: bfloat16 [1600, 6400], P('fsdp', 'tp'), may hold values from -0.15625 to 0.15625
- proj_weight: bfloat16 [6400, 1600], P('tp', 'fsdp'), may hold values from -0.078125 to 0.078125
- cotangent: bfloat16 [4, 1024, 1600], P('fsdp', 'ctx'), may hold values from -6 to 6
Outputs:
- block_output: bfloat16 [4, 1024, 1600], P('fsdp', 'ctx')
- grad_input: float32 [4, 1024, 1600], P('fsdp', 'ctx')
- grad_ln1_gain: float32 [1600], P(('fsdp', 'ctx'))
- grad_ln1_shift: float32 [1600], P(('fsdp', 'ctx'))
- grad_qkv_weight: float32 [1600, 4800], P(('fsdp', 'ctx'))
- grad_out_weight: float32 [1600, 1600], P(None, ('fsdp', 'ctx'))
- grad_ln2_gain: float32 [1600], P(('fsdp', 'ctx'))
- grad_ln2_shift: float32 [1600], P(('fsdp', 'ctx'))
- grad_fc_weight: float32 [1600, 6400], P(('fsdp', 'ctx'), 'tp')
- grad_proj_weight: float32 [6400, 1600], P('tp', ('fsdp', 'ctx'))
All inputs are finite; a program needn't handle non-finite values.
Results may differ from a plain program's by a relative error of at most 0.013.
The roundings to bfloat16 on the way count: a program that leaves them out, or rounds other values in their place, can miss the bound.
Values may be sent and summed in bfloat16 or wider, within the bound.
A program may use at most 320 MiB of HBM per device.

v0:
```python
import jax
import jax.numpy as jnp
from jax import lax
from jax.sharding import PartitionSpec as P

D = 1600
H = 25
HD = 64


norm_epsilon = 1e-05


def normalize(values, norm_gain, norm_shift):
    row_mean = jnp.mean(values, axis=-1, keepdims=True)
    centered = values - row_mean
    inv_std = lax.rsqrt(jnp.mean(centered * centered, axis=-1, keepdims=True) + norm_epsilon)
    normed = centered * inv_std
    return (normed * norm_gain + norm_shift, normed, inv_std)


def norm_back(upstream, normed, inv_std, norm_gain):
    scaled = upstream * norm_gain
    back_grad = inv_std * (
        scaled
        - jnp.mean(scaled, axis=-1, keepdims=True)
        - normed * jnp.mean(scaled * normed, axis=-1, keepdims=True)
    )
    return (back_grad, jnp.sum(upstream * normed, axis=(0, 1)), jnp.sum(upstream, axis=(0, 1)))


def masked_scores(queries, key_rows, query_seg, key_seg, query_pos):
    raw_scores = jnp.einsum("qhd,khd->hqk", queries, key_rows, preferred_element_type=jnp.float32)
    scores = raw_scores * queries.shape[-1] ** (-0.5)
    key_pos = jnp.arange(key_rows.shape[0], dtype=jnp.int32)
    allowed = (key_pos[None, :] <= query_pos[:, None]) & (key_seg[None, :] == query_seg[:, None])
    return jnp.where(allowed[None], scores, -1e30)


def attend(queries, key_rows, value_rows, query_seg, key_seg, query_pos):
    scores = masked_scores(queries, key_rows, query_seg, key_seg, query_pos)
    row_max = jnp.max(scores, axis=-1, keepdims=True)
    exponent = jnp.exp(scores - row_max)
    row_total = jnp.sum(exponent, axis=-1, keepdims=True)
    probabilities = (exponent / row_total).astype(jnp.bfloat16)
    attended = jnp.einsum(
        "hqk,khd->qhd", probabilities, value_rows, preferred_element_type=jnp.float32
    )
    return (attended, row_max + jnp.log(row_total))


def attend_back(
    queries, key_rows, value_rows, query_seg, key_seg, query_pos, log_total, grad_attended
):
    scores = masked_scores(queries, key_rows, query_seg, key_seg, query_pos)
    probabilities = jnp.exp(scores - log_total)
    grad_values = jnp.einsum(
        "hqk,qhd->khd",
        probabilities.astype(jnp.bfloat16),
        grad_attended,
        preferred_element_type=jnp.float32,
    )
    grad_probs = jnp.einsum(
        "qhd,khd->hqk", grad_attended, value_rows, preferred_element_type=jnp.float32
    )
    row_inner = jnp.sum(probabilities * grad_probs, axis=-1, keepdims=True)
    grad_raw = (probabilities * (grad_probs - row_inner) * queries.shape[-1] ** (-0.5)).astype(
        jnp.bfloat16
    )
    grad_query = jnp.einsum("hqk,khd->qhd", grad_raw, key_rows, preferred_element_type=jnp.float32)
    grad_keys = jnp.einsum("hqk,qhd->khd", grad_raw, queries, preferred_element_type=jnp.float32)
    return (grad_query, grad_keys, grad_values)


def slots_of(member, head_slots, tp_size):
    first_head = member * H // tp_size
    last_head = (member + 1) * H // tp_size
    wanted = first_head + jnp.arange(head_slots, dtype=jnp.int32)
    slot_heads = jnp.minimum(wanted, H - 1)
    slot_valid = (wanted < last_head).astype(jnp.float32)
    return (slot_heads, slot_valid)


def gelu_tanh(values):
    return jax.nn.gelu(values, approximate=True)


def local(
    block_input,
    segments,
    ln1_gain,
    ln1_shift,
    qkv_weight,
    out_weight,
    ln2_gain,
    ln2_shift,
    fc_weight,
    proj_weight,
    cotangent,
):
    tp_size = lax.axis_size("tp")
    tp_rank = lax.axis_index("tp")
    head_slots = (H + tp_size - 1) // tp_size
    slot_heads, slot_valid = slots_of(tp_rank, head_slots, tp_size)
    gathered = (
        lax.all_gather(qkv_weight, "fsdp", axis=0, tiled=True),
        lax.all_gather(out_weight, "fsdp", axis=1, tiled=True),
        lax.all_gather(fc_weight, "fsdp", axis=0, tiled=True),
        lax.all_gather(proj_weight, "fsdp", axis=1, tiled=True),
    )
    matrix = gathered[0]
    row_count = matrix.shape[0]
    query_key_value_weight = jnp.take(
        matrix.reshape(row_count, 3, H, HD), slot_heads, axis=2
    ).reshape(row_count, 3 * head_slots * HD)
    matrix = gathered[1]
    col_count = matrix.shape[1]
    contract_weight = jnp.take(matrix.reshape(H, HD, col_count), slot_heads, axis=0).reshape(
        head_slots * HD, col_count
    )
    expand_weight = gathered[2]
    attention_projection_weight = gathered[3]
    head_select_mask = jnp.repeat(slot_valid, HD).astype(jnp.bfloat16)
    contract_weight = contract_weight * head_select_mask[:, None]
    seq_count, local_len, model_width = block_input.shape
    input_f32 = block_input.astype(jnp.float32)
    hidden_one, normed_one, inv_one = normalize(input_f32, ln1_gain, ln1_shift)
    first_hidden_reduced = hidden_one.astype(jnp.bfloat16)
    qkv_values = jnp.einsum(
        "iwq,qr->iwr",
        first_hidden_reduced,
        query_key_value_weight,
        preferred_element_type=jnp.float32,
    ).astype(jnp.bfloat16)
    qkv_values = qkv_values.reshape(seq_count, local_len, 3, head_slots, HD)
    queries = qkv_values[:, :, 0]
    kv_local = jnp.stack([qkv_values[:, :, 1], qkv_values[:, :, 2]])
    seg_low = segments.astype(jnp.bfloat16)
    kv_all, seg_all = (
        lax.all_gather(kv_local, "ctx", axis=2, tiled=True),
        lax.all_gather(seg_low, "ctx", axis=1, tiled=True),
    )
    query_pos = lax.axis_index("ctx") * local_len + jnp.arange(local_len, dtype=jnp.int32)
    attended, log_total = lax.map(
        lambda entry: attend(entry[0], entry[1], entry[2], entry[3], entry[4], query_pos),
        (queries, kv_all[0], kv_all[1], seg_low, seg_all),
    )
    attention_output_reduced = attended.astype(jnp.bfloat16).reshape(
        seq_count, local_len, head_slots * HD
    )
    attn_sum = lax.psum(
        jnp.einsum(
            "qwa,ap->qwp",
            attention_output_reduced,
            contract_weight,
            preferred_element_type=jnp.float32,
        ),
        "tp",
    )
    residual_one = input_f32 + attn_sum
    hidden_two, normed_two, inv_two = normalize(residual_one, ln2_gain, ln2_shift)
    second_hidden_reduced = hidden_two.astype(jnp.bfloat16)
    pre_act = jnp.einsum(
        "whv,vi->whi", second_hidden_reduced, expand_weight, preferred_element_type=jnp.float32
    )
    activation, gelu_pull = jax.vjp(gelu_tanh, pre_act)
    activation_reduced = activation.astype(jnp.bfloat16)
    mlp_sum = lax.psum(
        jnp.einsum(
            "ojk,kg->ojg",
            activation_reduced,
            attention_projection_weight,
            preferred_element_type=jnp.float32,
        ).astype(jnp.bfloat16),
        "tp",
    ).astype(jnp.float32)
    result = (residual_one + mlp_sum).astype(jnp.bfloat16)
    grad_output = cotangent.astype(jnp.float32)
    projection_gradient = jnp.einsum(
        "xbi,xbm->im", activation_reduced, cotangent, preferred_element_type=jnp.float32
    )
    activation_gradient = jnp.einsum(
        "tua,ya->tuy", cotangent, attention_projection_weight, preferred_element_type=jnp.float32
    )
    preactivation_gradient = gelu_pull(activation_gradient)[0].astype(jnp.bfloat16)
    grad_fc = jnp.einsum(
        "atm,atk->mk",
        second_hidden_reduced,
        preactivation_gradient,
        preferred_element_type=jnp.float32,
    )
    grad_h2 = lax.psum(
        jnp.einsum(
            "kau,gu->kag", preactivation_gradient, expand_weight, preferred_element_type=jnp.float32
        ),
        "tp",
    )
    back_two, grad_g2, grad_s2 = norm_back(grad_h2, normed_two, inv_two, ln2_gain)
    grad_r1 = grad_output + back_two
    attention_gradient = grad_r1.astype(jnp.bfloat16)
    grad_out_local = jnp.einsum(
        "izy,izr->yr",
        attention_output_reduced * head_select_mask,
        attention_gradient,
        preferred_element_type=jnp.float32,
    )
    grad_attended = jnp.einsum(
        "gmi,ti->gmt", attention_gradient, contract_weight, preferred_element_type=jnp.float32
    )
    grad_attended = grad_attended.astype(jnp.bfloat16).reshape(seq_count, local_len, head_slots, HD)
    grad_query, grad_keys, grad_values = lax.map(
        lambda entry: attend_back(
            entry[0], entry[1], entry[2], entry[3], entry[4], query_pos, entry[5], entry[6]
        ),
        (queries, kv_all[0], kv_all[1], seg_low, seg_all, log_total, grad_attended),
    )
    kv_grad = lax.psum_scatter(
        jnp.stack([grad_keys, grad_values]).astype(jnp.bfloat16),
        "ctx",
        scatter_dimension=2,
        tiled=True,
    ).astype(jnp.float32)
    query_key_value_gradient = jnp.stack([grad_query, kv_grad[0], kv_grad[1]], axis=2).astype(
        jnp.bfloat16
    )
    query_key_value_gradient = query_key_value_gradient.reshape(
        seq_count, local_len, 3 * head_slots * HD
    )
    grad_qkv_local = jnp.einsum(
        "axy,axh->yh",
        first_hidden_reduced,
        query_key_value_gradient,
        preferred_element_type=jnp.float32,
    )
    grad_h1 = lax.psum(
        jnp.einsum(
            "cbz,iz->cbi",
            query_key_value_gradient,
            query_key_value_weight,
            preferred_element_type=jnp.float32,
        ),
        "tp",
    )
    back_one, grad_g1, grad_s1 = norm_back(grad_h1, normed_one, inv_one, ln1_gain)
    grad_total = grad_r1 + back_one
    qkv_full = (
        jnp.zeros((D, 3, H, HD), jnp.float32)
        .at[:, :, slot_heads, :]
        .add(grad_qkv_local.reshape(D, 3, head_slots, HD))
    )
    out_full = (
        jnp.zeros((H, HD, D), jnp.float32)
        .at[slot_heads]
        .add(grad_out_local.reshape(head_slots, HD, D))
    )
    partial_value = (
        lax.psum_scatter(
            qkv_full.reshape(D, 3 * H * HD), ("fsdp", "ctx"), scatter_dimension=0, tiled=True
        ),
        lax.psum_scatter(
            out_full.reshape(H * HD, D), ("fsdp", "ctx"), scatter_dimension=1, tiled=True
        ),
    )
    qkv_grad_out, out_grad_out = (
        lax.psum(partial_value[0].astype(jnp.bfloat16), "tp").astype(jnp.float32),
        lax.psum(partial_value[1].astype(jnp.bfloat16), "tp").astype(jnp.float32),
    )
    unit_sums = (
        lax.psum_scatter(grad_fc, ("fsdp", "ctx"), scatter_dimension=0, tiled=True),
        lax.psum_scatter(projection_gradient, ("fsdp", "ctx"), scatter_dimension=1, tiled=True),
        lax.psum_scatter(grad_g1, ("fsdp", "ctx"), scatter_dimension=0, tiled=True),
        lax.psum_scatter(grad_s1, ("fsdp", "ctx"), scatter_dimension=0, tiled=True),
        lax.psum_scatter(grad_g2, ("fsdp", "ctx"), scatter_dimension=0, tiled=True),
        lax.psum_scatter(grad_s2, ("fsdp", "ctx"), scatter_dimension=0, tiled=True),
    )
    return (
        result,
        grad_total,
        unit_sums[2],
        unit_sums[3],
        qkv_grad_out,
        out_grad_out,
        unit_sums[4],
        unit_sums[5],
        unit_sums[0],
        unit_sums[1],
    )


def solution(mesh):
    placed = (
        P("fsdp", "ctx", None),
        P("fsdp", "ctx"),
        P(),
        P(),
        P("fsdp", None),
        P(None, "fsdp"),
        P(),
        P(),
        P("fsdp", "tp"),
        P("tp", "fsdp"),
        P("fsdp", "ctx", None),
    )
    return jax.shard_map(
        local,
        mesh=mesh,
        in_specs=placed,
        out_specs=(
            P("fsdp", "ctx", None),
            P("fsdp", "ctx", None),
            P(("fsdp", "ctx")),
            P(("fsdp", "ctx")),
            P(("fsdp", "ctx"), None),
            P(None, ("fsdp", "ctx")),
            P(("fsdp", "ctx")),
            P(("fsdp", "ctx")),
            P(("fsdp", "ctx"), "tp"),
            P("tp", ("fsdp", "ctx")),
        ),
        check_vma=False,
    )
```

profile of v0, /device:TPU:0, one launch (start us, length us, event | category | flops | bytes accessed | tf_op | source)
XLA Modules:
  0.0 3262.2 jit_solution(14725272297948683888)
XLA Ops:
  9.3 269.9 %all-gather.6.cloned.1.call-done = bf16[1600,4800]{1,0:T(8,128)(2,1)} async-done(((bf16[400,4800]{1,0:T(8,128)(2,1)}), bf16[1600,4800]{1,0:T(8,128)(2,1)}) %all-gather.6.cloned.1.call-update) | async-done | bytes 15360016 | tf_op jit(solution)/shard_map/all_gather | solution.py:106
  279.3 22.4 copy.30
  301.6 13.5 copy.31
  315.1 10.7 gather_fusion
  325.8 7.5 select_bitcast_fusion
  333.3 7.3 copy.32
  340.6 6.0 convolution_convert_fusion
  348.0 8.2 all_gather.22
  356.6 21.8 all-gather.10.cloned.1.call-done
  378.4 9.6 copy.33
  388.0 5.2 gather_fusion.1
  393.2 3.7 select_multiply_fusion
  396.9 28.2 all-gather.8.cloned.1.call-done
  425.1 7.6 fusion.91
  432.7 7.3 fusion.7
  440.0 6.6 fusion.59
  453.8 16.0 all-reduce.20.cloned.1.call-done
  471.8 180.5 %all-gather.12.cloned.1.call-done = bf16[1600,3200]{1,0:T(8,128)(2,1)} async-done(((bf16[400,3200]{1,0:T(8,128)(2,1)}), bf16[1600,3200]{1,0:T(8,128)(2,1)}) %all-gather.12.cloned.1.call-update) | async-done | bytes 10240016 | tf_op jit(solution)/shard_map/all_gather | solution.py:108
  652.3 9.1 fusion.86
  661.4 170.5 %all-gather.14.cloned.1.call-done = bf16[3200,1600]{0,1:T(8,128)(2,1)} async-done(((bf16[3200,400]{0,1:T(8,128)(2,1)}), bf16[3200,1600]{0,1:T(8,128)(2,1)}) %all-gather.14.cloned.1.call-update) | async-done | bytes 10240016 | tf_op jit(solution)/shard_map/all_gather | solution.py:109
  831.8 9.8 fusion.26
  842.8 4.2 convolution_bitcast_fusion.2
  847.3 10.8 fusion.66
  858.1 9.2 fusion.84
  867.4 3.0 multiply_reduce_fusion.1
  873.7 8.5 fusion.48
  882.2 6.9 fusion.54
  889.0 26.9 fusion.51
  915.9 4.1 pad_maximum_fusion
  920.1 961.2 %fusion.88 = (f32[112,3200]{1,0:T(8,128)}, f32[3200,112]{0,1:T(8,128)S(1)}) fusion(f32[1600,3200]{1,0:T(8,128)} %fusion.84, f32[3200,1600]{0,1:T(8,128)} %fusion.66), kind=kCustom, calls=%all-reduce-scatter.3 | all-reduce-scatter fusion | flops 11468801 | bytes 43827712
  1889.4 2.7 collective-permute-start.4
  1894.3 25.5 fusion.55
  1921.2 8.4 convolution_bitcast_fusion
  1929.6 7.9 convolution_bitcast_fusion.1
  1937.6 11.4 copy.34
  1949.0 10.9 broadcast_in_dim.115
  1960.0 33.4 %scatter_fusion = f32[1600,3,25,64]{0,3,2,1:T(8,128)} fusion(f32[1600,3,25,64]{0,3,2,1:T(8,128)} %broadcast_in_dim.115, s32[13]{0:T(128)S(1)} %copy-done.27, f32[13,1600,3,64]{1,3,2,0:T(8,128)} %copy.34), kind=kCustom, calls=%fused_computation.2 | custom fusion | flops 3993600 | bytes 47923252 | tf_op jit(solution)/shard_map/scatter-add | solution.py:249
  1993.4 34.2 %copy.35 = f32[1600,4800]{1,0:T(8,128)} copy(f32[1600,4800]{0,1:T(8,128)} %bitcast.129) | data formatting | bytes 61440000 | tf_op jit(solution)/shard_map/reshape | solution.py:258
  2027.6 671.4 %fusion = f32[104,4800]{1,0:T(8,128)} fusion(f32[1600,4800]{1,0:T(8,128)} %copy.35), kind=kCustom, calls=%all-reduce-scatter | all-reduce-scatter fusion | flops 7987201 | bytes 32717312
  2702.9 8.9 fusion.27
  2711.8 3.4 fusion.63
  2715.2 5.1 broadcast_in_dim.116
  2720.3 15.3 scatter_fusion.1
  2735.6 9.3 concatenate.17
  2749.8 459.8 %all-reduce.27 = (bf16[1600,1600]{1,0:T(8,128)(2,1)}, f32[1600]{0:T(1024)S(1)}, f32[1600]{0:T(1024)S(1)}, f32[1600]{0:T(1024)S(1)}, f32[1600]{0:T(1024)S(1)}) all-reduce(f32[1600,1600]{1,0:T(8,128)} %bitcast.130, f32[1600]{0:T(1024)S(1)} %get-tuple-element.95, ...), channel_id=6, replica_groups=mesh['fsdp'=4,'ctx'=4,'tp'=2] {'fsdp','ctx'}, use_global_device_ids=true, to_apply=%region_24.25.clone | all-reduce | flops 2566400 | bytes 15411200
  3212.3 14.7 concatenate.18
  3227.0 13.9 concatenate.19
  3240.9 2.7 constant_dynamic-slice_fusion.1
  (140 shorter events, 50.2 us)
Async XLA Ops:
  7.2 1.6 copy-start.2
  7.2 272.1 %all-gather.6.cloned.1.call-start = ((), (), s32[]{:S(2)}) async-start(), calls=%async_computation.1 | async-start | bytes 19456000 | tf_op jit(solution)/shard_map/all_gather | solution.py:106
  7.9 370.5 %all-gather.10.cloned.1.call-start = ((), (), s32[]{:S(2)}) async-start(), calls=%async_computation.3 | async-start | bytes 6656000 | tf_op jit(solution)/shard_map/all_gather | solution.py:107
  8.7 416.4 %all-gather.8.cloned.1.call-start = ((), (), s32[]{:S(2)}) async-start(), calls=%async_computation.2 | async-start | bytes 4259840 | tf_op jit(solution)/shard_map/all_gather | solution.py:140
  8.7 292.9 %copy-start.26 = (s32[13]{0:T(128)}, s32[13]{0:T(128)S(1)}, u32[]{:S(2)}) copy-start(s32[13]{0:T(128)S(1)} %fusion.77) | copy-start | bytes 160
  333.3 7.3 copy-start.22
  333.3 7.3 copy-start.25
  346.6 78.5 %copy-start.17 = (bf16[256,2496]{0,1:T(8,128)(2,1)}, bf16[256,2496]{0,1:T(8,128)(2,1)S(1)}, u32[]{:S(2)}) copy-start(bf16[256,2496]{0,1:T(8,128)(2,1)S(1)} %convolution_convert_fusion) | copy-start | bytes 3833860
  346.6 1.3 copy-start.29
  347.9 121.9 %all-reduce.20.cloned.1.call-start = ((), (), s32[]{:S(2)}) async-start(), calls=%async_computation.4 | async-start | bytes 3276800 | tf_op jit(solution)/shard_map/psum | solution.py:151
  432.7 7.3 copy-start.12
  440.0 6.6 copy-start.7
  449.1 1.8 copy-start.28
  449.1 203.1 %all-gather.12.cloned.1.call-start = ((), (), s32[]{:S(2)}) async-start(), calls=%async_computation.5 | async-start | bytes 12800000 | tf_op jit(solution)/shard_map/all_gather | solution.py:108
  449.7 382.1 %all-gather.14.cloned.1.call-start = ((), (), s32[]{:S(2)}) async-start(), calls=%async_computation.6 | async-start | bytes 12800000 | tf_op jit(solution)/shard_map/all_gather | solution.py:109
  450.3 417.0 %all-reduce.22.cloned.1.call-start = ((), (), s32[]{:S(2)}) async-start(), calls=%async_computation.7 | async-start | bytes 3276800 | tf_op jit(solution)/shard_map/psum | solution.py:192
  452.8 199.4 %copy-start.19 = (f32[1600]{0:T(1024)S(1)}, f32[1600]{0:T(1024)}, u32[]{:S(2)}) copy-start(f32[1600]{0:T(1024)} %param.17) | copy-start | bytes 19204
  452.8 199.4 %copy-start.21 = (f32[1600]{0:T(1024)S(1)}, f32[1600]{0:T(1024)}, u32[]{:S(2)}) copy-start(f32[1600]{0:T(1024)} %param.18) | copy-start | bytes 19204
  471.5 398.9 %copy-start = (f32[1,256,1600]{1,2,0:T(8,128)}, f32[1,256,1600]{1,2,0:T(8,128)S(1)}, u32[]{:S(2)}) copy-start(f32[1,256,1600]{1,2,0:T(8,128)S(1)} %get-tuple-element.114) | copy-start | bytes 4915204
  471.7 360.1 %copy-start.11 = (bf16[1,256,1600]{1,2,0:T(8,128)(2,1)S(1)}, bf16[1,256,1600]{1,2,0:T(8,128)(2,1)}, u32[]{:S(2)}) copy-start(bf16[1,256,1600]{1,2,0:T(8,128)(2,1)} %param.21) | copy-start | bytes 2457604
  831.8 11.0 copy-start.3
  841.6 1.2 copy-start.15
  847.0 1072.8 %reduce-scatter.9.cloned.1.call-start = ((), (), s32[]{:S(2)}) async-start(), calls=%async_computation.8 | async-start | bytes 4259840 | tf_op jit(solution)/shard_map/reduce_scatter | solution.py:217
  847.3 10.9 copy-start.16
  867.4 3.0 copy-start.10
  870.4 2.4 copy-start.8
  870.9 2.7 copy-start.4
  873.7 8.5 copy-start.13
  920.1 1827.3 %all-reduce.24.cloned.1.call-start = ((), (), s32[]{:S(2)}) async-start(), calls=%async_computation.9 | async-start | bytes 3276800 | tf_op jit(solution)/shard_map/psum | solution.py:235
  1883.5 1328.8 %collective-permute-start.1 = (f32[112,3200]{1,0:T(8,128)}, f32[112,3200]{1,0:T(8,128)}, u32[]{:S(2)}, u32[]{:S(2)}) collective-permute-start(f32[112,3200]{1,0:T(8,128)} %get-tuple-element.111), channel_id=1, source_target_pairs={{0,2},{2,4},{4,6},{6,8},{8,10},{10,12},{12,14},{14,16},{16,18},{18... | collective-permute-start | bytes 4300808
  1887.0 1340.0 %collective-permute-start.3 = (f32[3200,112]{0,1:T(8,128)S(1)}, f32[3200,112]{0,1:T(8,128)}, u32[]{:S(2)}, u32[]{:S(2)}) collective-permute-start(f32[3200,112]{0,1:T(8,128)S(1)} %get-tuple-element.112), channel_id=1, source_target_pairs={{0,2},{2,4},{4,6},{6,8},{8,10},{10,12},{12,14},{14,16},{16,18},{18... | collective-permute-start | bytes 4300808
  1889.4 1337.6 %collective-permute-start.4 = (f32[3200,68]{0,1:T(8,128)}, f32[3200,68]{0,1:T(8,128)}, u32[]{:S(2)}, u32[]{:S(2)}) collective-permute-start(f32[3200,68]{0,1:T(8,128)} %slice.43), channel_id=1, source_target_pairs={{0,4},{2,6},{4,8},{6,10},{8,12},{10,14},{12,16},{14,18},{16,20},{1... | collective-permute-start | bytes 2611208
  1892.1 1320.2 %collective-permute-start.2 = (f32[68,3200]{1,0:T(8,128)}, f32[68,3200]{1,0:T(8,128)}, u32[]{:S(2)}, u32[]{:S(2)}) collective-permute-start(f32[68,3200]{1,0:T(8,128)} %slice.42), channel_id=1, source_target_pairs={{0,4},{2,6},{4,8},{6,10},{8,12},{10,14},{12,16},{14,18},{16,20},{1... | collective-permute-start | bytes 2611208
  1937.6 1312.5 %all-reduce.26.cloned.1.call-start = ((), (), s32[]{:S(2)}) async-start(), calls=%async_computation.10 | async-start | bytes 4481024 | tf_op jit(solution)/shard_map/psum | solution.py:266
  1949.0 11.0 copy-start.27
  2701.2 10.6 copy-start.5
  2701.2 10.6 copy-start.14
  2701.2 34.4 %collective-permute-start = (bf16[60,4800]{1,0:T(8,128)(2,1)}, bf16[60,4800]{1,0:T(8,128)(2,1)S(1)}, u32[]{:S(2)}, u32[]{:S(2)}) collective-permute-start(bf16[60,4800]{1,0:T(8,128)(2,1)} %slice.41), channel_id=1, source_target_pairs={{0,2},{2,4},{4,6},{6,8},{8,10},{10,12},{12,14},{14,16},{16,18},{18... | collective-permute-start | bytes 1728008
  2744.9 4.8 copy-start.23
  2744.9 4.8 copy-start.24
  3240.9 7.6 copy-start.6
  3240.9 7.6 copy-start.9
  3246.1 4.0 copy-start.1
  3250.1 2.3 copy-start.20
  3250.1 3.4 copy-start.18
Sparse Core Ops, SparseCore 0:
  9.6 269.6 all-gather.5
  280.8 97.5 all-gather.9
  380.8 44.2 all-gather.7
  449.3 20.4 all-reduce.19
  471.2 181.0 all-gather.11
  653.7 178.0 all-gather.13
  847.2 18.6 all-reduce.21
  920.2 149.3 reduce-scatter.8
  1937.7 32.3 all-reduce.23
  3211.8 20.5 all-reduce.25
where the time goes:
time: 3270 us; the launch traced here: 3260 us
  blocking collectives  2100 us (64%)
  waiting for transfers between devices  689 us (21%)
  local copies, waits for them, and re-layouts  192 us (6%)
  matrix products  163 us (5%)
  other arithmetic  87.7 us (3%)
    unnamed x3, blocking collectives  2090 us
    all_gather x1, waiting for transfers between devices, local(): lax.all_gather(qkv_weight, 'fsdp', axis=0, tiled=True)  270 us
    all_gather x1, waiting for transfers between devices, local(): lax.all_gather(fc_weight, 'fsdp', axis=0, tiled=True)  181 us
    all_gather x1, waiting for transfers between devices, local(): lax.all_gather(proj_weight, 'fsdp', axis=1, tiled=True)  170 us
  transfers between devices with their start and end apart: 15, of which 6 were waited for; matrix products, arithmetic and copies ran while one was open for 61% of the time, Pallas kernels for 0%

commit v1 on v0

v1 whole, which is shorter than its diff:
```python
import jax
import jax.numpy as jnp
from jax import lax
from jax.sharding import PartitionSpec as P

H = 25
HD = 64
EPS = 1e-05
BF = jnp.bfloat16
F32 = jnp.float32
PLANE = ("ctx", "tp")


def dot(lhs, rhs, dims):
    return lax.dot_general(lhs, rhs, (dims, ((), ())), preferred_element_type=F32)


def moments(values):
    centered = values - jnp.mean(values, axis=-1, keepdims=True)
    inv_std = lax.rsqrt(jnp.mean(centered * centered, axis=-1, keepdims=True) + EPS)
    return centered * inv_std, inv_std


def norm_back(upstream, normed, inv_std, gain):
    scaled = upstream * gain
    return inv_std * (
        scaled
        - jnp.mean(scaled, axis=-1, keepdims=True)
        - normed * jnp.mean(scaled * normed, axis=-1, keepdims=True)
    )


def gelu_tanh(values):
    return jax.nn.gelu(values, approximate=True)


def masked_scores(queries, keys, seg):
    length = queries.shape[0]
    scores = jnp.einsum("qhd,khd->hqk", queries, keys, preferred_element_type=F32) * HD ** (-0.5)
    pos = jnp.arange(length, dtype=jnp.int32)
    allowed = (pos[None, :] <= pos[:, None]) & (seg[None, :] == seg[:, None])
    return jnp.where(allowed[None], scores, -1e30)


def attend(queries, keys, values, seg):
    scores = masked_scores(queries, keys, seg)
    row_max = jnp.max(scores, axis=-1, keepdims=True)
    exponent = jnp.exp(scores - row_max)
    total = jnp.sum(exponent, axis=-1, keepdims=True)
    probs = (exponent / total).astype(BF)
    attended = jnp.einsum("hqk,khd->qhd", probs, values, preferred_element_type=F32)
    return attended.astype(BF), row_max + jnp.log(total)


def attend_back(queries, keys, values, seg, lse, grad):
    probs = jnp.exp(masked_scores(queries, keys, seg) - lse)
    grad_v = jnp.einsum("hqk,qhd->khd", probs.astype(BF), grad, preferred_element_type=F32)
    grad_p = jnp.einsum("qhd,khd->hqk", grad, values, preferred_element_type=F32)
    inner = jnp.sum(probs * grad_p, axis=-1, keepdims=True)
    raw = (probs * (grad_p - inner) * HD ** (-0.5)).astype(BF)
    grad_q = jnp.einsum("hqk,khd->qhd", raw, keys, preferred_element_type=F32)
    grad_k = jnp.einsum("hqk,qhd->khd", raw, queries, preferred_element_type=F32)
    return grad_q, grad_k, grad_v


def build(mesh):
    ctx_n, tp_n = mesh.shape["ctx"], mesh.shape["tp"]
    members = ctx_n * tp_n
    slots = -(-H // members)
    starts = [m * H // members for m in range(members + 1)]
    counts = [starts[m + 1] - starts[m] for m in range(members)]
    width = slots * HD

    def local(x, segments, g1, b1, wqkv, wout, g2, b2, wfc, wproj, cot):
        x, cot = x[0], cot[0]
        rows, model = x.shape
        tp_i, ctx_i = lax.axis_index("tp"), lax.axis_index("ctx")
        member = ctx_i * tp_n + tp_i
        own = rows // tp_n
        head0 = member * H // members
        head_n = (member + 1) * H // members - head0
        valid = jnp.arange(width, dtype=jnp.int32) < head_n * HD

        def cols(matrix, start, size):
            return lax.dynamic_slice_in_dim(matrix, start, size, 1)

        def rows_of(matrix, start, size):
            return lax.dynamic_slice_in_dim(matrix, start, size, 0)

        wq = jnp.concatenate([cols(wqkv, p * H * HD + head0 * HD, width) for p in range(3)], axis=1)
        wq = lax.all_gather(wq, "fsdp", axis=0, tiled=True)
        part = model // members
        wo = lax.all_gather(rows_of(wout, member * part, part), "fsdp", axis=1, tiled=True)
        wo = lax.all_gather(wo, PLANE, axis=0, tiled=True)
        hidden = wfc.shape[1] // ctx_n
        wf = lax.all_gather(cols(wfc, ctx_i * hidden, hidden), "fsdp", axis=0, tiled=True)
        wp = lax.all_gather(rows_of(wproj, ctx_i * hidden, hidden), "fsdp", axis=1, tiled=True)

        def to_plane(v):
            return lax.all_gather(v, PLANE, axis=0, tiled=True)

        def from_plane(v):
            return lax.psum_scatter(v, PLANE, scatter_dimension=0, tiled=True)

        x_own = rows_of(x, tp_i * own, own)
        cot_own = rows_of(cot, tp_i * own, own)
        x_all = to_plane(x_own)
        cot_all = to_plane(cot_own)
        seg = lax.all_gather(segments[0], "ctx", axis=0, tiled=True)
        length = x_all.shape[0]

        n1_all, _ = moments(x_all.astype(F32))
        h1 = (n1_all * g1 + b1).astype(BF)
        qkv = dot(h1, wq, ((1,), (0,))).astype(BF).reshape(length, 3, slots, HD)
        q, k, v = qkv[:, 0], qkv[:, 1], qkv[:, 2]
        attended, lse = attend(q, k, v, seg)
        attended = attended.reshape(length, width)
        spread = lax.all_to_all(attended, PLANE, 0, 1, tiled=True)
        att_own = jnp.concatenate(
            [spread[:, m * width : m * width + counts[m] * HD] for m in range(members)], axis=1
        )
        x_own_f32 = x_own.astype(F32)
        r1 = x_own_f32 + dot(att_own, wo, ((1,), (0,)))
        n2, s2 = moments(r1)
        h2 = to_plane((n2 * g2 + b2).astype(BF))
        pre = dot(h2, wf, ((1,), (0,)))
        act, pull = jax.vjp(gelu_tanh, pre)
        act = act.astype(BF)
        mlp = from_plane(dot(act, wp, ((1,), (0,))))
        out = lax.all_gather((r1 + mlp).astype(BF), "tp", axis=0, tiled=True)

        grad_proj = dot(act, cot_all, ((0,), (0,)))
        grad_pre = pull(dot(cot_all, wp, ((1,), (1,))))[0].astype(BF)
        grad_fc = dot(h2, grad_pre, ((0,), (0,)))
        grad_h2 = from_plane(dot(grad_pre, wf, ((1,), (1,))))
        grad_r1 = cot_own.astype(F32) + norm_back(grad_h2, n2, s2, g2)
        grad_att = to_plane(grad_r1.astype(BF))
        wo_mine = rows_of(wo, head0 * HD, width)
        grad_out = dot(attended, grad_att, ((0,), (0,)))
        grad_attended = jnp.where(valid, dot(grad_att, wo_mine, ((1,), (1,))), 0.0).astype(BF)
        dq, dk, dv = attend_back(q, k, v, seg, lse, grad_attended.reshape(length, slots, HD))
        dqkv = jnp.stack([dq, dk, dv], axis=1).astype(BF).reshape(length, 3 * width)
        grad_qkv = dot(h1, dqkv, ((0,), (0,)))
        grad_h1 = from_plane(dot(dqkv, wq, ((1,), (1,))))
        n1, s1 = moments(x_own_f32)
        grad_x = grad_r1 + norm_back(grad_h1, n1, s1, g1)
        grad_x = lax.all_gather(grad_x, "tp", axis=0, tiled=True)

        def over_fsdp(v, dim):
            return lax.psum_scatter(v, "fsdp", scatter_dimension=dim, tiled=True)

        fc_out = lax.all_to_all(over_fsdp(grad_fc, 0), "ctx", 0, 1, tiled=True)
        proj_out = lax.all_to_all(over_fsdp(grad_proj, 1), "ctx", 1, 0, tiled=True)
        gq = over_fsdp(grad_qkv, 0).astype(BF)
        gq = gq.reshape(ctx_n, gq.shape[0] // ctx_n, 3 * width)
        gq = lax.all_gather(lax.all_to_all(gq, "ctx", 0, 0, tiled=True), "tp", axis=1)
        gq = gq.reshape((members,) + gq.shape[2:])
        qkv_out = jnp.concatenate(
            [
                gq[m][:, p * width : p * width + counts[m] * HD]
                for p in range(3)
                for m in range(members)
            ],
            axis=1,
        ).astype(F32)
        go = over_fsdp(grad_out, 1).astype(BF)
        go = lax.all_to_all(go, "ctx", 1, 0, tiled=True)
        go = lax.all_gather(go.reshape(ctx_n, width, go.shape[1]), "tp", axis=1)
        go = go.reshape((members,) + go.shape[2:])
        out_out = jnp.concatenate([go[m][: counts[m] * HD] for m in range(members)], axis=0)
        out_out = out_out.astype(F32)
        sums = jnp.stack(
            [
                jnp.sum(grad_h1 * n1, axis=0),
                jnp.sum(grad_h1, axis=0),
                jnp.sum(grad_h2 * n2, axis=0),
                jnp.sum(grad_h2, axis=0),
            ]
        )
        sums = lax.psum_scatter(
            lax.psum(sums, "tp"), ("fsdp", "ctx"), scatter_dimension=1, tiled=True
        )
        return (
            out[None],
            grad_x[None],
            sums[0],
            sums[1],
            qkv_out,
            out_out,
            sums[2],
            sums[3],
            fc_out,
            proj_out,
        )

    return local


def solution(mesh):
    placed = (
        P("fsdp", "ctx", None),
        P("fsdp", "ctx"),
        P(),
        P(),
        P("fsdp", None),
        P(None, "fsdp"),
        P(),
        P(),
        P("fsdp", "tp"),
        P("tp", "fsdp"),
        P("fsdp", "ctx", None),
    )
    both = ("fsdp", "ctx")
    return jax.shard_map(
        build(mesh),
        mesh=mesh,
        in_specs=placed,
        out_specs=(
            P("fsdp", "ctx", None),
            P("fsdp", "ctx", None),
            P(both),
            P(both),
            P(both, None),
            P(None, both),
            P(both),
            P(both),
            P(both, "tp"),
            P("tp", both),
        ),
        check_vma=False,
    )
```

time: 3270 us -> 1060 us (0.32)
  blocking collectives: 2100 us -> 130 us
  local copies, waits for them, and re-layouts: 192 us -> 43.3 us
  other arithmetic: 87.7 us -> 32 us
  waiting for transfers between devices: 689 us -> 644 us
    unnamed x3 -> x1, blocking collectives: 2090 us -> 75.6 us
    all_gather x5 -> x10, waiting for transfers between devices: 671 us -> 239 us  [the longest x4 83.9 us: to_plane(): return lax.all_gather(v, PLANE, axis=0, tiled=True)]
    reduce_scatter x1 -> x7, waiting for transfers between devices: 0.02 us -> 405 us  [the longest x4 220 us: over_fsdp(): return lax.psum_scatter(v, 'fsdp', scatter_dimension=dim, tiled=True)]
    unnamed x74 -> x55, local copies, waits for them, and re-layouts: 55.5 us -> 5.49 us
    scatter-add x2 -> x0, other arithmetic: 48.7 us -> none  [the longest x1 33.4 us: local(): qkv_full = jnp.zeros((D, 3, H, HD), jnp.float32).at[:, :, slot_heads, :]....]
    reshape x2 -> x3, local copies, waits for them, and re-layouts: 47.7 us -> 1.32 us  [the longest x1 0.95 us: local(): gq = gq.reshape(ctx_n, gq.shape[0] // ctx_n, 3 * width)]
  transfers between devices with their start and end apart: 15 -> 21, of which waited for: 6 -> 13; matrix products, arithmetic and copies ran while one was open for 61% -> 18% of each run, Pallas kernels for 0% -> 0%
where the time goes in v1:
time: 1060 us; the launch traced here: 1050 us
  waiting for transfers between devices  644 us (61%)
  matrix products  161 us (15%)
  blocking collectives  130 us (12%)
  local copies, waits for them, and re-layouts  43.3 us (4%)
  other arithmetic  32 us (3%)
  starting transfers between devices  26.2 us (2%)
  between operations  15.7 us (1%)
    reduce_scatter x4, waiting for transfers between devices, over_fsdp(): return lax.psum_scatter(v, 'fsdp', scatter_dimension=dim, tiled=True)  220 us
    reduce_scatter x3, waiting for transfers between devices, from_plane(): return lax.psum_scatter(v, PLANE, scatter_dimension=0, tiled=True)  185 us
    all_gather x4, waiting for transfers between devices, to_plane(): return lax.all_gather(v, PLANE, axis=0, tiled=True)  83.9 us
    dot_general x12, matrix products, dot(): lax.dot_general(lhs, rhs, (dims, ((), ())), preferred_element_type=F32)  79.7 us
    unnamed x1, blocking collectives  75.6 us
    all_gather x1, waiting for transfers between devices, local(): lax.all_gather(rows_of(wproj, ctx_i * hidden, hidden), 'fsdp', axis=1, ti...  53.2 us
    all_gather x1, waiting for transfers between devices, local(): lax.all_gather(cols(wfc, ctx_i * hidden, hidden), 'fsdp', axis=0, tiled=T...  52 us
    all_gather x1, waiting for transfers between devices, local(): wq = lax.all_gather(wq, 'fsdp', axis=0, tiled=True)  50.2 us
  transfers between devices with their start and end apart: 21, of which 13 were waited for; matrix products, arithmetic and copies ran while one was open for 18% of the time, Pallas kernels for 0%

profile of v1, /device:TPU:0, one launch (start us, length us, event | category | flops | bytes accessed | tf_op | source)
XLA Modules:
  0.0 1052.5 jit_solution(6024526135875657321)
XLA Ops:
  12.9 21.7 %all_gather.48 = bf16[200,1600]{0,1:T(8,128)(2,1)S(1)} all-gather(bf16[200,400]{0,1:T(8,128)(2,1)S(1)} %constant_dynamic-slice_fusion.3), channel_id=1, replica_groups=mesh['fsdp'=4,'ctx'=4,'tp'=2] {'fsdp'}, dimensions={1}, use_global_device_ids=true | all-gather | bytes 800000 | tf_op jit(solution)/shard_map/all_gather | solution.py:93
  37.0 8.2 all-gather.1
  46.5 2.7 convert_reduce_fusion
  50.4 50.2 %all-gather.16.cloned.1.call-done = bf16[1600,768]{1,0:T(8,128)(2,1)} async-done(((bf16[400,768]{1,0:T(8,128)(2,1)}), bf16[1600,768]{1,0:T(8,128)(2,1)}) %all-gather.16.cloned.1.call-update) | async-done | bytes 2457616 | tf_op jit(solution)/shard_map/all_gather | solution.py:91
  100.6 6.1 convolution_convert_fusion
  106.8 7.5 fusion.91
  114.3 8.0 fusion.4
  122.3 8.3 fusion.48
  130.7 17.1 %all_to_all.78 = bf16[8,128,256]{1,2,0:T(8,128)(2,1)S(1)} all-to-all(bf16[8,128,256]{1,2,0:T(8,128)(2,1)S(1)} %copy.96), channel_id=1, replica_groups=mesh['fsdp'=4,'ctx'=4,'tp'=2] {'ctx','tp'}, dimensions={0} | all-to-all | bytes 1048576 | tf_op jit(solution)/shard_map/all_to_all | solution.py:118
  148.0 4.7 fusion.92
  157.6 52.0 %all-gather.22.cloned.1.call-done = bf16[1600,800]{1,0:T(8,128)(2,1)} async-done(((bf16[400,800]{1,0:T(8,128)(2,1)}), bf16[1600,800]{1,0:T(8,128)(2,1)}) %all-gather.22.cloned.1.call-update) | async-done | bytes 2560016 | tf_op jit(solution)/shard_map/all_gather | solution.py:96
  209.6 34.3 %all-gather.20.cloned.1.call-done = bf16[1024,1600]{0,1:T(8,128)(2,1)} async-done(((bf16[128,1600]{0,1:T(8,128)(2,1)}), bf16[1024,1600]{0,1:T(8,128)(2,1)}) %all-gather.20.cloned.1.call-update) | async-done | bytes 3276816 | tf_op jit(solution)/shard_map/all_gather | solution.py:100
  243.9 7.6 fusion.93
  251.5 53.2 %all-gather.24.cloned.1.call-done = bf16[800,1600]{0,1:T(8,128)(2,1)} async-done(((bf16[800,400]{0,1:T(8,128)(2,1)}), bf16[800,1600]{0,1:T(8,128)(2,1)}) %all-gather.24.cloned.1.call-update) | async-done | bytes 2560016 | tf_op jit(solution)/shard_map/all_gather | solution.py:97
  304.8 34.5 %all-gather.32.cloned.1.call-done = bf16[1,1024,1600]{1,2,0:T(8,128)(2,1)} async-done(((bf16[1,128,1600]{1,2,0:T(8,128)(2,1)}), bf16[1,1024,1600]{1,2,0:T(8,128)(2,1)}) %all-gather.32.cloned.1.call-update) | async-done | bytes 3276816 | tf_op jit(solution)/shard_map/all_gather | solution.py:100
  339.2 9.0 fusion.31
  349.4 5.5 fusion.96
  354.9 63.0 %reduce-scatter.11.cloned.1.call-done = f32[128,1600]{0,1:T(8,128)} async-done(((f32[1024,1600]{0,1:T(8,128)}), f32[128,1600]{0,1:T(8,128)}) %reduce-scatter.11.cloned.1.call-update) | async-done | bytes 819216 | tf_op jit(solution)/shard_map/reduce_scatter | solution.py:103
  422.0 9.8 reduce-scatter.21.cloned.1.call-start
  431.8 9.1 fusion.32
  441.0 14.4 %all-gather.26.cloned.1.call-done = bf16[1024,1600]{0,1:T(8,128)(2,1)} async-done(((bf16[128,1600]{0,1:T(8,128)(2,1)}), bf16[1024,1600]{0,1:T(8,128)(2,1)}) %all-gather.26.cloned.1.call-update) | async-done | bytes 3276816 | tf_op jit(solution)/shard_map/all_gather | solution.py:100
  455.5 3.3 fusion.47
  458.8 10.0 fusion.71
  468.8 23.6 %fusion.55 = bf16[1024,1,4,64]{0,3,2,1:T(8,128)(2,1)} fusion(f32[4,1024,1024]{1,2,0:T(8,128)} %fusion.71, f32[4,1024,1024]{1,2,0:T(8,128)} %get-tuple-element.69, f32[4,1024]{1,0:T(4,128)S(1)} %log_add_fusion, bf16[1024,3,4,64]{0,3,2,1:T(8,128)(2,1)} %bitcast.215), kind=kOutput, calls=%fused_computation.52 | convolution fusion | flops 566498304 | bytes 68190208 | tf_op jit(solution)/shard_map/hqk,khd->qhd/dot_general | solution.py:61
  492.4 23.7 %fusion.52 = bf16[1024,1,4,64]{0,3,2,1:T(8,128)(2,1)} fusion(f32[4,1024,1024]{1,2,0:T(8,128)} %fusion.71, f32[4,1024,1024]{1,2,0:T(8,128)} %get-tuple-element.69, f32[4,1024]{1,0:T(4,128)S(1)} %log_add_fusion, bf16[1024,3,4,64]{0,3,2,1:T(8,128)(2,1)} %bitcast.216), kind=kOutput, calls=%fused_computation.51 | convolution fusion | flops 566498304 | bytes 68190208 | tf_op jit(solution)/shard_map/hqk,qhd->khd/dot_general | solution.py:62
  516.1 8.7 fusion.49
  526.2 4.6 fusion.97
  531.1 9.3 fusion.78
  540.4 8.4 fusion.95
  549.0 7.9 fusion.79
  556.9 4.1 fusion.94
  561.4 2.8 all_to_all.69
  564.1 4.3 all-to-all-start.4
  568.8 57.5 %reduce-scatter.13.cloned.1.call-done = f32[128,1600]{0,1:T(8,128)} async-done(((f32[1024,1600]{0,1:T(8,128)}), f32[128,1600]{0,1:T(8,128)}) %reduce-scatter.13.cloned.1.call-update) | async-done | bytes 819216 | tf_op jit(solution)/shard_map/reduce_scatter | solution.py:103
  628.2 64.3 %reduce-scatter.9.cloned.1.call-done = f32[128,1600]{0,1:T(8,128)} async-done(((f32[1024,1600]{0,1:T(8,128)}), f32[128,1600]{0,1:T(8,128)}) %reduce-scatter.9.cloned.1.call-update) | async-done | bytes 819216 | tf_op jit(solution)/shard_map/reduce_scatter | solution.py:103
  692.5 2.9 fusion.68
  695.4 101.2 %reduce-scatter.19.cloned.1.call-done = f32[400,800]{1,0:T(8,128)} async-done(((f32[1600,800]{1,0:T(8,128)}), f32[400,800]{1,0:T(8,128)}) %reduce-scatter.19.cloned.1.call-update) | async-done | bytes 1280016 | tf_op jit(solution)/shard_map/reduce_scatter | solution.py:150
  799.2 3.7 all-to-all-start.3
  802.9 84.9 %reduce-scatter.15.cloned.1.call-done = f32[400,768]{1,0:T(8,128)} async-done(((f32[1600,768]{1,0:T(8,128)}), f32[400,768]{1,0:T(8,128)}) %reduce-scatter.15.cloned.1.call-update) | async-done | bytes 1228816 | tf_op jit(solution)/shard_map/reduce_scatter | solution.py:150
  890.1 3.7 all-to-all-start.1
  893.8 33.8 %reduce-scatter.17.cloned.1.call-done = f32[256,400]{0,1:T(8,128)} async-done(((f32[256,1600]{0,1:T(8,128)}), f32[256,400]{0,1:T(8,128)}) %reduce-scatter.17.cloned.1.call-update) | async-done | bytes 409616 | tf_op jit(solution)/shard_map/reduce_scatter | solution.py:150
  929.3 3.7 all-to-all-start.2
  935.3 3.0 copy.119
  938.3 2.9 all_to_all.72
  942.6 2.9 all_to_all.68
  952.3 75.6 %all-reduce = f32[4,1600]{1,0:T(4,128)S(1)} all-reduce(f32[4,1600]{1,0:T(4,128)S(1)} %pad_maximum_fusion.2), channel_id=10, replica_groups=mesh['fsdp'=4,'ctx'=4,'tp'=2] {'fsdp','ctx'}, use_global_device_ids=true, to_apply=%region_21.22.clone | all-reduce | flops 6400 | bytes 51200
  1037.5 3.2 concatenate.14
  1040.7 2.8 convert_element_type.83
  (167 shorter events, 53.3 us)
Async XLA Ops:
  7.2 28.6 %copy-start = (bf16[400,3200]{1,0:T(8,128)(2,1)S(1)}, bf16[400,3200]{1,0:T(8,128)(2,1)}, u32[]{:S(2)}) copy-start(bf16[400,3200]{1,0:T(8,128)(2,1)} %param.19) | copy-start | bytes 7680004
  7.2 39.3 %all-gather.30.cloned.1.call-start = ((), (), s32[]{:S(2)}) async-start(), calls=%async_computation.26 | async-start | bytes 3686400 | tf_op jit(solution)/shard_map/all_gather | solution.py:100
  9.3 91.3 %all-gather.16.cloned.1.call-start = ((), (), s32[]{:S(2)}) async-start(), calls=%async_computation.12 | async-start | bytes 3072000 | tf_op jit(solution)/shard_map/all_gather | solution.py:91
  11.7 25.3 %copy-start.15 = (s32[1,256]{1,0:T(1,128)S(1)}, s32[1,256]{1,0:T(1,128)}, u32[]{:S(2)}) copy-start(s32[1,256]{1,0:T(1,128)} %param.12) | copy-start | bytes 3076
  11.7 136.3 %all-gather.18.cloned.1.call-start = ((), (), s32[]{:S(2)}) async-start(), calls=%async_computation.13 | async-start | bytes 5990400 | tf_op jit(solution)/shard_map/all_gather | solution.py:94
  35.7 173.8 %all-gather.22.cloned.1.call-start = ((), (), s32[]{:S(2)}) async-start(), calls=%async_computation.15 | async-start | bytes 3584000 | tf_op jit(solution)/shard_map/all_gather | solution.py:96
  37.0 206.9 %all-gather.20.cloned.1.call-start = ((), (), s32[]{:S(2)}) async-start(), calls=%async_computation.14 | async-start | bytes 3686400 | tf_op jit(solution)/shard_map/all_gather | solution.py:100
  45.9 54.7 %copy-start.13 = (f32[1600]{0:T(1024)S(1)}, f32[1600]{0:T(1024)}, u32[]{:S(2)}) copy-start(f32[1600]{0:T(1024)} %param.13) | copy-start | bytes 19204
  46.5 2.9 copy-start.3
  46.5 54.1 %copy-start.18 = (f32[1600]{0:T(1024)S(1)}, f32[1600]{0:T(1024)}, u32[]{:S(2)}) copy-start(f32[1600]{0:T(1024)} %param.14) | copy-start | bytes 19204
  106.8 15.5 %copy-start.11 = (bf16[1024,768]{0,1:T(8,128)(2,1)}, bf16[1024,768]{0,1:T(8,128)(2,1)S(1)}, u32[]{:S(2)}) copy-start(bf16[1024,768]{0,1:T(8,128)(2,1)S(1)} %convolution_convert_fusion) | copy-start | bytes 4718596
  130.5 17.5 %copy-start.2 = (bf16[1,128,1600]{1,2,0:T(8,128)(2,1)S(1)}, bf16[1,128,1600]{1,2,0:T(8,128)(2,1)}, u32[]{:S(2)}) copy-start(bf16[1,128,1600]{1,2,0:T(8,128)(2,1)} %get-tuple-element.19) | copy-start | bytes 1228804
  148.0 5.0 copy-start.12
  148.0 5.0 copy-start.14
  152.7 4.0 copy-start.5
  154.2 150.5 %all-gather.24.cloned.1.call-start = ((), (), s32[]{:S(2)}) async-start(), calls=%async_computation.16 | async-start | bytes 3584000 | tf_op jit(solution)/shard_map/all_gather | solution.py:97
  156.6 182.6 %all-gather.32.cloned.1.call-start = ((), (), s32[]{:S(2)}) async-start(), calls=%async_computation.27 | async-start | bytes 3686400 | tf_op jit(solution)/shard_map/all_gather | solution.py:100
  157.5 260.3 %reduce-scatter.11.cloned.1.call-start = ((), (), s32[]{:S(2)}) async-start(), calls=%async_computation.18 | async-start | bytes 7372800 | tf_op jit(solution)/shard_map/reduce_scatter | solution.py:103
  339.2 10.2 copy-start.16
  348.2 1.2 copy-start.20
  354.9 100.6 %all-gather.26.cloned.1.call-start = ((), (), s32[]{:S(2)}) async-start(), calls=%async_computation.19 | async-start | bytes 3686400 | tf_op jit(solution)/shard_map/all_gather | solution.py:100
  422.0 139.3 %reduce-scatter.21.cloned.1.call-start = ((), (), s32[]{:S(2)}) async-start(), calls=%async_computation.25 | async-start | bytes 7168000 | tf_op jit(solution)/shard_map/reduce_scatter | solution.py:150
  440.9 185.4 %reduce-scatter.13.cloned.1.call-start = ((), (), s32[]{:S(2)}) async-start(), calls=%async_computation.20 | async-start | bytes 7372800 | tf_op jit(solution)/shard_map/reduce_scatter | solution.py:103
  516.1 8.7 copy-start.9
  516.1 8.7 copy-start.10
  516.1 10.1 copy-start.17
  525.0 1.1 copy-start.8
  530.8 161.7 %reduce-scatter.9.cloned.1.call-start = ((), (), s32[]{:S(2)}) async-start(), calls=%async_computation.17 | async-start | bytes 7372800 | tf_op jit(solution)/shard_map/reduce_scatter | solution.py:103
  540.4 256.2 %reduce-scatter.19.cloned.1.call-start = ((), (), s32[]{:S(2)}) async-start(), calls=%async_computation.24 | async-start | bytes 7168000 | tf_op jit(solution)/shard_map/reduce_scatter | solution.py:150
  548.9 338.9 %reduce-scatter.15.cloned.1.call-start = ((), (), s32[]{:S(2)}) async-start(), calls=%async_computation.22 | async-start | bytes 6144000 | tf_op jit(solution)/shard_map/reduce_scatter | solution.py:150
  556.8 370.7 %reduce-scatter.17.cloned.1.call-start = ((), (), s32[]{:S(2)}) async-start(), calls=%async_computation.23 | async-start | bytes 2048000 | tf_op jit(solution)/shard_map/reduce_scatter | solution.py:150
  561.3 131.2 %copy-start.4 = (f32[128,1600]{0,1:T(8,128)S(1)}, f32[128,1600]{0,1:T(8,128)}, u32[]{:S(2)}) copy-start(f32[128,1600]{0,1:T(8,128)} %reduce-scatter.11.cloned.1.call-done) | copy-start | bytes 2457604
  561.3 131.2 %copy-start.6 = (bf16[1,256,1600]{1,2,0:T(8,128)(2,1)S(1)}, bf16[1,256,1600]{1,2,0:T(8,128)(2,1)}, u32[]{:S(2)}) copy-start(bf16[1,256,1600]{1,2,0:T(8,128)(2,1)} %param.21) | copy-start | bytes 2457604
  564.1 235.1 %all-to-all-start.4 = ((f32[800,4,100]{0,2,1:T(8,128)}), f32[800,4,100]{0,2,1:T(8,128)}, u32[]{:S(2)}, u32[]{:S(2)}) async-start(f32[800,4,100]{0,2,1:T(8,128)} %all_to_all.69), calls=%async_computation.11 | async-start | bytes 2981888 | tf_op jit(solution)/shard_map/all_to_all | solution.py:153
  568.5 462.5 %all-gather.28.cloned.1.call-start = ((), (), s32[]{:S(2)}) async-start(), calls=%async_computation.21 | async-start | bytes 2457600 | tf_op jit(solution)/shard_map/all_gather | solution.py:147
  799.2 90.9 %all-to-all-start.3 = ((f32[4,100,800]{2,1,0:T(8,128)}), f32[4,100,800]{2,1,0:T(8,128)S(1)}, u32[]{:S(2)}, u32[]{:S(2)}) async-start(f32[4,100,800]{2,1,0:T(8,128)} %all_to_all.65), calls=%async_computation.9 | async-start | bytes 2981888 | tf_op jit(solution)/shard_map/all_to_all | solution.py:152
  889.2 44.9 %copy-start.19 = (u32[32]{0:T(128)S(1)}, u32[32]{0:T(128)}, u32[]{:S(2)}) copy-start(u32[32]{0:T(128)} %constant.100) | copy-start | bytes 388
  890.1 39.2 %all-to-all-start.1 = ((bf16[4,100,768]{2,1,0:T(8,128)(2,1)}), bf16[4,100,768]{2,1,0:T(8,128)(2,1)S(1)}, u32[]{:S(2)}, u32[]{:S(2)}) async-start(bf16[4,100,768]{2,1,0:T(8,128)(2,1)} %reshape.173), calls=%async_computation.5 | async-start | bytes 1277952 | tf_op jit(solution)/shard_map/all_to_all | solution.py:156
  929.3 16.2 %all-to-all-start.2 = ((bf16[256,4,100]{0,2,1:T(8,128)(2,1)}), bf16[256,4,100]{0,2,1:T(8,128)(2,1)S(1)}, u32[]{:S(2)}, u32[]{:S(2)}) async-start(bf16[256,4,100]{0,2,1:T(8,128)(2,1)} %all_to_all.62), calls=%async_computation.7 | async-start | bytes 425984 | tf_op jit(solution)/shard_map/all_to_all | solution.py:167
  933.0 98.0 %all-gather.34.cloned.1.call-start = ((), (), s32[]{:S(2)}) async-start(), calls=%async_computation.28 | async-start | bytes 1843200 | tf_op jit(solution)/shard_map/all_gather | solution.py:156
  1037.5 8.0 copy-start.1
  1040.7 3.7 copy-start.7
Sparse Core Ops, SparseCore 0:
  10.5 36.0 all-gather.29
  48.7 51.8 all-gather.15
  103.1 44.1 all-gather.17
  149.3 60.2 all-gather.21
  211.8 31.9 all-gather.19
  245.9 58.8 all-gather.23
  307.2 31.9 all-gather.31
  355.0 62.8 reduce-scatter.10
  422.1 33.2 all-gather.25
  457.7 101.7 reduce-scatter.20
  562.9 63.3 reduce-scatter.12
  629.6 62.8 reduce-scatter.8
  694.8 101.7 reduce-scatter.18
  798.8 88.9 reduce-scatter.14
  890.5 36.9 reduce-scatter.16
  929.5 8.4 all-gather.27
  939.9 10.4 all-gather.33

commit v2 on v1

--- a/solution.py
+++ b/solution.py
@@ -1,6 +1,10 @@
+import functools
+
 import jax
 import jax.numpy as jnp
 from jax import lax
+from jax.experimental import pallas as pl
+from jax.experimental.pallas import tpu as pltpu
 from jax.sharding import PartitionSpec as P
 
 H = 25
@@ -9,6 +13,230 @@
 BF = jnp.bfloat16
 F32 = jnp.float32
 PLANE = ("ctx", "tp")
+
+
+VMEM = pl.BlockSpec(memory_space=pltpu.VMEM)
+MESH = pl.DeviceIdType.MESH
+
+
+def flip(index, stride):
+    return index + stride * (1 - 2 * ((index // stride) % 2))
+
+
+def strides_of(ctx_n, tp_i):
+    bits = ctx_n.bit_length() - 1
+    plain = [1 << b for b in range(bits)]
+    turned = plain[1:] + plain[:1]
+    return [a + (b - a) * tp_i for a, b in zip(plain, turned)]
+
+
+def greet(partners):
+    barrier = pltpu.get_barrier_semaphore()
+    for who in partners:
+        pl.semaphore_signal(barrier, inc=1, device_id=who, device_id_type=MESH)
+    pl.semaphore_wait(barrier, len(partners))
+
+
+def remote(src, dst, send, recv, who):
+    return pltpu.make_async_remote_copy(
+        src_ref=src, dst_ref=dst, send_sem=send, recv_sem=recv, device_id=who, device_id_type=MESH
+    )
+
+
+def comm_params(ident, limit):
+    return pltpu.CompilerParams(
+        collective_id=ident, has_side_effects=True, vmem_limit_bytes=limit
+    )
+
+
+def gather_kernel(ctx_n, tp_n, own_ref, all_ref, send, recv, sib_send, sib_recv, local_sem):
+    rows = own_ref.shape[0]
+    ctx_i, tp_i = lax.axis_index("ctx"), lax.axis_index("tp")
+    strides = strides_of(ctx_n, tp_i)
+    sibling = {"tp": 1 - tp_i}
+    greet([{"ctx": flip(ctx_i, s)} for s in strides] + [sibling])
+
+    def place(c):
+        return all_ref.at[pl.ds(pl.multiple_of((c * tp_n + tp_i) * rows, rows), rows)]
+
+    mine = pltpu.make_async_copy(own_ref, place(ctx_i), local_sem)
+    mine.start()
+    held = [ctx_i]
+    pending = []
+    to_sibling = remote(own_ref, place(ctx_i), sib_send.at[0], sib_recv.at[0], sibling)
+    to_sibling.start()
+    pending.append(to_sibling)
+    slot = 0
+    for step, stride in enumerate(strides):
+        copies = []
+        for position, c in enumerate(held):
+            src = own_ref if position == 0 else place(c)
+            copy = remote(src, place(c), send.at[slot], recv.at[slot], {"ctx": flip(ctx_i, stride)})
+            copy.start()
+            copies.append(copy)
+            slot += 1
+        fresh = [flip(c, stride) for c in held]
+        for copy, c in zip(copies, fresh):
+            copy.wait_recv()
+            passed = len(pending)
+            onward = remote(place(c), place(c), sib_send.at[passed], sib_recv.at[passed], sibling)
+            onward.start()
+            pending.append(onward)
+        for copy in copies:
+            copy.wait_send()
+        held = held + fresh
+    for copy in pending:
+        copy.wait()
+    mine.wait()
+
+
+def plane_gather(own, ctx_n, tp_n, ident):
+    rows, columns = own.shape
+    return pl.pallas_call(
+        functools.partial(gather_kernel, ctx_n, tp_n),
+        out_shape=jax.ShapeDtypeStruct((rows * ctx_n * tp_n, columns), own.dtype),
+        in_specs=[VMEM],
+        out_specs=VMEM,
+        scratch_shapes=[
+            pltpu.SemaphoreType.DMA((ctx_n - 1,)),
+            pltpu.SemaphoreType.DMA((ctx_n - 1,)),
+            pltpu.SemaphoreType.DMA((ctx_n,)),
+            pltpu.SemaphoreType.DMA((ctx_n,)),
+            pltpu.SemaphoreType.DMA,
+        ],
+        compiler_params=comm_params(ident, 32 << 20),
+        cost_estimate=pl.CostEstimate(flops=0, bytes_accessed=30 << 20, transcendentals=0),
+        name=f"plane_gather_{ident}",
+    )(own)
+
+
+def exchange_kernel(ctx_n, tp_n, src_ref, dst_ref, send, recv, local_sem):
+    members = ctx_n * tp_n
+    rows = src_ref.shape[0] // members
+    me = lax.axis_index("ctx") * tp_n + lax.axis_index("tp")
+
+    def block(member):
+        return src_ref.at[pl.ds(pl.multiple_of(member * rows, rows), rows)]
+
+    others = [lax.rem(me + shift, members) for shift in range(1, members)]
+    ids = [{"ctx": other // tp_n, "tp": other % tp_n} for other in others]
+    greet(ids)
+    copies = [
+        remote(block(other), dst_ref.at[me], send.at[i], recv.at[i], who)
+        for i, (other, who) in enumerate(zip(others, ids))
+    ]
+    for copy in copies:
+        copy.start()
+    mine = pltpu.make_async_copy(block(me), dst_ref.at[me], local_sem)
+    mine.start()
+    for copy in copies:
+        copy.wait()
+    mine.wait()
+
+
+def plane_exchange(values, ctx_n, tp_n, ident):
+    members = ctx_n * tp_n
+    rows, columns = values.shape
+    return pl.pallas_call(
+        functools.partial(exchange_kernel, ctx_n, tp_n),
+        out_shape=jax.ShapeDtypeStruct((members, rows // members, columns), values.dtype),
+        in_specs=[VMEM],
+        out_specs=VMEM,
+        scratch_shapes=[
+            pltpu.SemaphoreType.DMA((members - 1,)),
+            pltpu.SemaphoreType.DMA((members - 1,)),
+            pltpu.SemaphoreType.DMA,
+        ],
+        compiler_params=comm_params(ident, 16 << 20),
+        cost_estimate=pl.CostEstimate(flops=0, bytes_accessed=15 << 20, transcendentals=0),
+        name=f"plane_exchange_{ident}",
+    )(values)
+
+
+def reduce_kernel(
+    ctx_n, tp_n, turned, lhs_ref, rhs_ref, out_ref,
+    part, near, got, sib_send, sib_recv, send, recv,
+):
+    rows = out_ref.shape[0]
+    ctx_i, tp_i = lax.axis_index("ctx"), lax.axis_index("tp")
+    strides = strides_of(ctx_n, tp_i)
+    sibling = {"tp": 1 - tp_i}
+    greet([{"ctx": flip(ctx_i, s)} for s in strides] + [sibling])
+    contract = ((1,), (1,)) if turned else ((1,), (0,))
+    to_sibling, onward = {}, {}
+    bits = len(strides)
+
+    def common(r):
+        turn = sum(1 << ((b + 1) % bits) for b in range(bits) if r >> b & 1)
+        return r + (turn - r) * tp_i
+
+    def first(r):
+        c = ctx_i
+        for b, stride in enumerate(strides):
+            if r >> b & 1:
+                c = flip(c, stride)
+        pair = lhs_ref[pl.ds(pl.multiple_of(c * tp_n * rows, tp_n * rows), tp_n * rows), :]
+        part[r] = dot(pair, rhs_ref[...], contract).reshape(tp_n, rows, rhs_ref.shape[0 if turned else 1])
+        to_sibling[r] = remote(
+            part.at[r, 1 - tp_i], near.at[common(r)],
+            sib_send.at[r], sib_recv.at[common(r)], sibling,
+        )
+        to_sibling[r].start()
+
+    def second(r):
+        to_sibling[r].wait_recv()
+        total = part[r, tp_i] + near[common(r)]
+        high = r.bit_length() - 1
+        for b in range(high + 1, len(strides)):
+            slot = (1 << b) - 1 + r
+            onward[(1 << b) + r].wait_recv()
+            total = total + got[slot]
+        if r:
+            near[common(r)] = total
+            slot = r - 1
+            onward[r] = remote(
+                near.at[common(r)], got.at[slot], send.at[slot], recv.at[slot],
+                {"ctx": flip(ctx_i, strides[high])},
+            )
+            onward[r].start()
+        else:
+            out_ref[...] = total
+
+    order = list(range(ctx_n - 1, -1, -1))
+    for i, r in enumerate(order):
+        first(r)
+        if i:
+            second(order[i - 1])
+    second(order[-1])
+    for copy in list(to_sibling.values()) + list(onward.values()):
+        copy.wait_send()
+
+
+def plane_reduce(lhs, rhs, ctx_n, tp_n, turned, ident):
+    members = ctx_n * tp_n
+    rows = lhs.shape[0] // members
+    columns = rhs.shape[0 if turned else 1]
+    inner = lhs.shape[1]
+    return pl.pallas_call(
+        functools.partial(reduce_kernel, ctx_n, tp_n, turned),
+        out_shape=jax.ShapeDtypeStruct((rows, columns), F32),
+        in_specs=[VMEM, VMEM],
+        out_specs=VMEM,
+        scratch_shapes=[
+            pltpu.VMEM((ctx_n, tp_n, rows, columns), F32),
+            pltpu.VMEM((ctx_n, rows, columns), F32),
+            pltpu.VMEM((ctx_n - 1, rows, columns), F32),
+            pltpu.SemaphoreType.DMA((ctx_n,)),
+            pltpu.SemaphoreType.DMA((ctx_n,)),
+            pltpu.SemaphoreType.DMA((ctx_n - 1,)),
+            pltpu.SemaphoreType.DMA((ctx_n - 1,)),
+        ],
+        compiler_params=comm_params(ident, 48 << 20),
+        cost_estimate=pl.CostEstimate(
+            flops=2 * lhs.shape[0] * inner * columns, bytes_accessed=60 << 20, transcendentals=0
+        ),
+        name=f"plane_reduce_{ident}",
+    )(lhs, rhs)
 
 
 def dot(lhs, rhs, dims):
@@ -96,16 +324,16 @@
         wf = lax.all_gather(cols(wfc, ctx_i * hidden, hidden), "fsdp", axis=0, tiled=True)
         wp = lax.all_gather(rows_of(wproj, ctx_i * hidden, hidden), "fsdp", axis=1, tiled=True)
 
-        def to_plane(v):
-            return lax.all_gather(v, PLANE, axis=0, tiled=True)
-
-        def from_plane(v):
-            return lax.psum_scatter(v, PLANE, scatter_dimension=0, tiled=True)
+        def to_plane(v, ident):
+            return plane_gather(v, ctx_n, tp_n, ident)
+
+        def from_plane(lhs, rhs, turned, ident):
+            return plane_reduce(lhs, rhs, ctx_n, tp_n, turned, ident)
 
         x_own = rows_of(x, tp_i * own, own)
         cot_own = rows_of(cot, tp_i * own, own)
-        x_all = to_plane(x_own)
-        cot_all = to_plane(cot_own)
+        x_all = to_plane(x_own, 0)
+        cot_all = to_plane(cot_own, 1)
         seg = lax.all_gather(segments[0], "ctx", axis=0, tiled=True)
         length = x_all.shape[0]
 
@@ -115,33 +343,35 @@
         q, k, v = qkv[:, 0], qkv[:, 1], qkv[:, 2]
         attended, lse = attend(q, k, v, seg)
         attended = attended.reshape(length, width)
-        spread = lax.all_to_all(attended, PLANE, 0, 1, tiled=True)
+        spread = plane_exchange(attended, ctx_n, tp_n, 2)
         att_own = jnp.concatenate(
-            [spread[:, m * width : m * width + counts[m] * HD] for m in range(members)], axis=1
+            [spread[m][:, : counts[m] * HD] for m in range(members)], axis=1
         )
         x_own_f32 = x_own.astype(F32)
         r1 = x_own_f32 + dot(att_own, wo, ((1,), (0,)))
         n2, s2 = moments(r1)
-        h2 = to_plane((n2 * g2 + b2).astype(BF))
+        h2 = to_plane((n2 * g2 + b2).astype(BF), 3)
         pre = dot(h2, wf, ((1,), (0,)))
         act, pull = jax.vjp(gelu_tanh, pre)
         act = act.astype(BF)
-        mlp = from_plane(dot(act, wp, ((1,), (0,))))
+        mlp = lax.psum_scatter(
+            dot(act, wp, ((1,), (0,))), PLANE, scatter_dimension=0, tiled=True
+        )
         out = lax.all_gather((r1 + mlp).astype(BF), "tp", axis=0, tiled=True)
 
         grad_proj = dot(act, cot_all, ((0,), (0,)))
         grad_pre = pull(dot(cot_all, wp, ((1,), (1,))))[0].astype(BF)
         grad_fc = dot(h2, grad_pre, ((0,), (0,)))
-        grad_h2 = from_plane(dot(grad_pre, wf, ((1,), (1,))))
+        grad_h2 = from_plane(grad_pre, wf, True, 4)
         grad_r1 = cot_own.astype(F32) + norm_back(grad_h2, n2, s2, g2)
-        grad_att = to_plane(grad_r1.astype(BF))
+        grad_att = to_plane(grad_r1.astype(BF), 5)
         wo_mine = rows_of(wo, head0 * HD, width)
         grad_out = dot(attended, grad_att, ((0,), (0,)))
         grad_attended = jnp.where(valid, dot(grad_att, wo_mine, ((1,), (1,))), 0.0).astype(BF)
         dq, dk, dv = attend_back(q, k, v, seg, lse, grad_attended.reshape(length, slots, HD))
         dqkv = jnp.stack([dq, dk, dv], axis=1).astype(BF).reshape(length, 3 * width)
         grad_qkv = dot(h1, dqkv, ((0,), (0,)))
-        grad_h1 = from_plane(dot(dqkv, wq, ((1,), (1,))))
+        grad_h1 = from_plane(dqkv, wq, True, 6)
         n1, s1 = moments(x_own_f32)
         grad_x = grad_r1 + norm_back(grad_h1, n1, s1, g1)
         grad_x = lax.all_gather(grad_x, "tp", axis=0, tiled=True)
@@ -177,9 +407,9 @@
                 jnp.sum(grad_h2, axis=0),
             ]
         )
-        sums = lax.psum_scatter(
-            lax.psum(sums, "tp"), ("fsdp", "ctx"), scatter_dimension=1, tiled=True
-        )
+        share = model // (lax.axis_size("fsdp") * ctx_n)
+        place = lax.axis_index("fsdp") * ctx_n + ctx_i
+        sums = cols(lax.psum(sums, ("fsdp", "ctx", "tp")), place * share, share)
         return (
             out[None],
             grad_x[None],

time: 1060 us -> 741 us (0.70)
  waiting for transfers between devices: 644 us -> 169 us
  Pallas kernels: 0 us -> 203 us
  blocking collectives: 130 us -> 88.2 us
  local copies, waits for them, and re-layouts: 43.3 us -> 73.4 us
  matrix products: 161 us -> 147 us
    pallas_call x0 -> x7, Pallas kernels: none -> 203 us  [the longest x4 106 us: plane_gather(): pl.pallas_call(functools.partial(gather_kernel, ctx_n, tp_n), out_shape=j...]
    reduce_scatter x3 -> x1, waiting for transfers between devices: 185 us -> 9.29 us  [local(): lax.psum_scatter(dot(act, wp, ((1,), (0,))), PLANE, scatter_dimension=0,...]
    reduce_scatter x4, waiting for transfers between devices: 220 us -> 128 us  [over_fsdp(): return lax.psum_scatter(v, 'fsdp', scatter_dimension=dim, tiled=True)]
    all_gather x4 -> x0, waiting for transfers between devices: 83.9 us -> none  [to_plane(): return lax.all_gather(v, PLANE, axis=0, tiled=True)]
    unnamed x1 -> x0, blocking collectives: 75.6 us -> none
    all_gather x1, waiting for transfers between devices: 52 us -> 0.01 us  [local(): lax.all_gather(cols(wfc, ctx_i * hidden, hidden), 'fsdp', axis=0, tiled=T...]
    all_gather x1, waiting for transfers between devices: 50.2 us -> 0.01 us  [local(): wq = lax.all_gather(wq, 'fsdp', axis=0, tiled=True)]
    psum x1, blocking collectives: 2.44 us -> 47.3 us  [local(): sums = cols(lax.psum(sums, ('fsdp', 'ctx', 'tp')), place * share, share)]
  transfers between devices with their start and end apart: 21 -> 15, of which waited for: 13 -> 4; matrix products, arithmetic and copies ran while one was open for 18% -> 25% of each run, Pallas kernels for 0% -> 28%
where the time goes in v2:
time: 741 us; the launch traced here: 736 us
  Pallas kernels  203 us (27%)
  waiting for transfers between devices  169 us (23%)
  matrix products  147 us (20%)
  blocking collectives  88.2 us (12%)
  local copies, waits for them, and re-layouts  73.4 us (10%)
  other arithmetic  25.6 us (3%)
  starting transfers between devices  15.9 us (2%)
  between operations  14.9 us (2%)
    reduce_scatter x4, waiting for transfers between devices, over_fsdp(): return lax.psum_scatter(v, 'fsdp', scatter_dimension=dim, tiled=True)  128 us
    pallas_call x4, Pallas kernels, plane_gather(): pl.pallas_call(functools.partial(gather_kernel, ctx_n, tp_n), out_shape=j...  106 us
    pallas_call x2, Pallas kernels, plane_reduce(): pl.pallas_call(functools.partial(reduce_kernel, ctx_n, tp_n, turned), out...  88 us
    dot_general x10, matrix products, dot(): lax.dot_general(lhs, rhs, (dims, ((), ())), preferred_element_type=F32)  66.6 us
    psum x1, blocking collectives, local(): sums = cols(lax.psum(sums, ('fsdp', 'ctx', 'tp')), place * share, share)  47.3 us
    all_gather x1, waiting for transfers between devices, local(): lax.all_gather(rows_of(wproj, ctx_i * hidden, hidden), 'fsdp', axis=1, ti...  31.7 us
    all_gather x1, blocking collectives, local(): lax.all_gather(rows_of(wout, member * part, part), 'fsdp', axis=1, tiled=...  28.5 us
    dot_general x1, matrix products, attend_back(): jnp.einsum('hqk,qhd->khd', raw, queries, preferred_element_type=F32)  24.1 us
  transfers between devices with their start and end apart: 15, of which 4 were waited for; matrix products, arithmetic and copies ran while one was open for 25% of the time, Pallas kernels for 28%

profile of v2, /device:TPU:0, one launch (start us, length us, event | category | flops | bytes accessed | tf_op | source)
XLA Modules:
  0.0 736.5 jit_solution(9041383716937959268)
XLA Ops:
  10.9 28.5 %all_gather.35 = bf16[200,1600]{0,1:T(8,128)(2,1)S(1)} all-gather(bf16[200,400]{0,1:T(8,128)(2,1)S(1)} %constant_dynamic-slice_fusion.4), channel_id=1, replica_groups=mesh['fsdp'=4,'ctx'=4,'tp'=2] {'fsdp'}, dimensions={1}, use_global_device_ids=true | all-gather | bytes 800000 | tf_op jit(solution)/shard_map/all_gather | solution.py:321
  41.9 2.4 constant_dynamic-slice_fusion.2
  44.4 7.9 %all-gather = s32[1,1024]{1,0:T(1,128)S(1)} all-gather(s32[1,256]{1,0:T(1,128)S(1)} %copy-done.36), channel_id=2, replica_groups=mesh['fsdp'=4,'ctx'=4,'tp'=2] {'ctx'}, dimensions={1}, use_global_device_ids=true | all-gather | bytes 5120 | tf_op jit(solution)/shard_map/all_gather | solution.py:337
  56.9 22.2 %plane_gather_0.1 = bf16[1024,1600]{1,0:T(8,128)(2,1)S(1)} custom-call(bf16[128,1600]{1,0:T(8,128)(2,1)S(1)} %bitcast.155), custom_call_target="tpu_custom_call" | custom-call | bytes 31457280 | tf_op jit(solution)/shard_map/plane_gather_0/pallas_call | solution.py:95
  80.7 38.2 %plane_gather_1.1 = bf16[1024,1600]{1,0:T(8,128)(2,1)S(1)} custom-call(bf16[128,1600]{1,0:T(8,128)(2,1)S(1)} %bitcast.156), custom_call_target="tpu_custom_call" | custom-call | bytes 31457280 | tf_op jit(solution)/shard_map/plane_gather_1/pallas_call | solution.py:95
  120.7 5.3 convolution_convert_fusion
  126.0 7.7 %fusion.77 = (f32[4,1024]{1,0:T(4,128)S(1)}, f32[4,1024,1024]{1,2,0:T(8,128)}) fusion(bf16[1024,3,4,64]{0,3,2,1:T(8,128)(2,1)S(1)} %bitcast.167, pred[1024,1024]{0,1:T(8,128)(4,1)S(1)} %copy-done.19), kind=kOutput, calls=%fused_computation.137 | convolution fusion | flops 549449728 | bytes 18890752 | tf_op jit(solution)/shard_map/qhd,khd->hqk/dot_general | solution.py:267
  133.7 8.0 %fusion.4 = f32[4,1024]{1,0:T(4,128)S(1)} fusion(f32[4,1024,1024]{1,2,0:T(8,128)} %get-tuple-element.148, f32[4,1024]{1,0:T(4,128)S(1)} %get-tuple-element.147), kind=kLoop, calls=%fused_computation.8 | loop fusion | flops 8384512 | bytes 16809984 | tf_op jit(solution)/shard_map/reduce_sum | solution.py:277
  141.8 8.3 %fusion.36 = bf16[4,64,1024]{2,1,0:T(8,128)(2,1)} fusion(f32[4,1024,1024]{1,2,0:T(8,128)} %get-tuple-element.148, f32[4,1024]{1,0:T(4,128)S(1)} %fusion.4, f32[4,1024]{1,0:T(4,128)S(1)} %get-tuple-element.147, bf16[1024,3,4,64]{0,3,2,1:T(8,128)(2,1)S(1)} %bitcast.168), kind=kOutput, calls=%fused_computation.39 | convolution fusion | flops 549715968 | bytes 17858560 | tf_op jit(solution)/shard_map/hqk,khd->qhd/dot_general | solution.py:279
  153.1 8.9 %plane_exchange_2.1 = bf16[8,128,256]{2,1,0:T(8,128)(2,1)S(1)} custom-call(bf16[1024,256]{1,0:T(8,128)(2,1)S(1)} %copy-done.9), custom_call_target="tpu_custom_call" | custom-call | bytes 15728640 | tf_op jit(solution)/shard_map/plane_exchange_2/pallas_call | solution.py:140
  164.7 3.8 fusion.78
  169.7 21.6 %plane_gather_3.1 = bf16[1024,1600]{1,0:T(8,128)(2,1)S(1)} custom-call(bf16[128,1600]{1,0:T(8,128)(2,1)S(1)} %add_convert_fusion.2.own_ref), custom_call_target="tpu_custom_call" | custom-call | bytes 31457280 | tf_op jit(solution)/shard_map/plane_gather_3/pallas_call | solution.py:95
  193.0 8.9 %fusion.79 = (f32[1024,800]{0,1:T(8,128)}, f32[1024,800]{0,1:T(8,128)}) fusion(bf16[1024,1600]{1,0:T(8,128)(2,1)} %copy-done.7, bf16[1600,800]{1,0:T(8,128)(2,1)} %all-gather.14.cloned.1.call-done.rhs_ref), kind=kOutput, calls=%fused_computation.139 | convolution fusion | flops 2622259200 | bytes 12390400 | tf_op jit(solution)/shard_map/dot_general | solution.py:243
  201.9 4.9 copy.216
  206.7 4.9 copy.219
  211.6 31.7 %all-gather.16.cloned.1.call-done = bf16[800,1600]{0,1:T(8,128)(2,1)} async-done(((bf16[800,400]{0,1:T(8,128)(2,1)}), bf16[800,1600]{0,1:T(8,128)(2,1)}) %all-gather.16.cloned.1.call-update) | async-done | bytes 2560016 | tf_op jit(solution)/shard_map/all_gather | solution.py:325
  243.3 12.0 %add_convert_fusion = (bf16[1024,800]{1,0:T(8,128)(2,1)}, bf16[1024,800]{1,0:T(8,128)(2,1)S(1)}) fusion(f32[1024,800]{1,0:T(8,128)} %copy.216, f32[1024,800]{1,0:T(8,128)} %copy.219, bf16[1024,1600]{1,0:T(8,128)(2,1)} %copy-done.5, bf16[800,1600]{0,1:T(8,128)(2,1)} %all-gather.16.cloned.1.call-done), kind=kOutput, calls=%fused_computation.26 | convolution fusion | flops 2638643200 | bytes 15667200 | tf_op jit(solution)/shard_map/dot_general | solution.py:243
  256.4 6.0 fusion.80
  262.7 9.1 %fusion.82 = f32[1600,800]{1,0:T(8,128)} fusion(bf16[1024,1600]{1,0:T(8,128)(2,1)} %copy-done.7, bf16[1024,800]{1,0:T(8,128)(2,1)} %get-tuple-element.90.lhs_ref), kind=kOutput, calls=%fused_computation.142 | convolution fusion | flops 2621440000 | bytes 10035200 | tf_op jit(solution)/shard_map/dot_general | solution.py:243
  272.6 2.2 copy-done.10
  276.5 53.5 %plane_reduce_4.1 = f32[128,1600]{1,0:T(8,128)S(1)} custom-call(bf16[1024,800]{1,0:T(8,128)(2,1)S(1)} %copy-done.12, bf16[1600,800]{1,0:T(8,128)(2,1)S(1)} %copy-done.10), custom_call_target="tpu_custom_call" | custom-call | flops 2621440000 | bytes 62914560 | tf_op jit(solution)/shard_map/plane_reduce_4/pallas_call | solution.py:220
  331.3 9.3 %reduce-scatter.6.cloned.1.call-done = f32[128,1600]{1,0:T(8,128)} async-done(((f32[1024,1600]{1,0:T(8,128)}), f32[128,1600]{1,0:T(8,128)}) %reduce-scatter.6.cloned.1.call-update) | async-done | bytes 819216 | tf_op jit(solution)/shard_map/reduce_scatter | solution.py:357
  340.6 3.3 fusion.67
  343.9 23.7 %plane_gather_5.1 = bf16[1024,1600]{1,0:T(8,128)(2,1)} custom-call(bf16[128,1600]{1,0:T(8,128)(2,1)S(1)} %get-tuple-element.88.own_ref), custom_call_target="tpu_custom_call" | custom-call | bytes 31457280 | tf_op jit(solution)/shard_map/plane_gather_5/pallas_call | solution.py:95
  367.6 3.5 fusion.26
  371.9 8.1 %fusion.58 = f32[4,1024,1024]{1,2,0:T(8,128)} fusion(bf16[1024,4,64]{0,2,1:T(8,128)(2,1)S(1)} %bitcast.161, bf16[1024,3,4,64]{0,3,2,1:T(8,128)(2,1)S(1)} %bitcast.171), kind=kOutput, calls=%fused_computation.70 | convolution fusion | flops 536870912 | bytes 17825792 | tf_op jit(solution)/shard_map/qhd,khd->hqk/dot_general | solution.py:286
  380.1 23.6 %fusion.43 = bf16[1024,1,4,64]{0,3,2,1:T(8,128)(2,1)} fusion(f32[4,1024,1024]{1,2,0:T(8,128)} %fusion.58, f32[4,1024,1024]{1,2,0:T(8,128)} %get-tuple-element.148, f32[4,1024]{1,0:T(4,128)S(1)} %log_add_fusion, bf16[1024,3,4,64]{0,3,2,1:T(8,128)(2,1)} %bitcast.169), kind=kOutput, calls=%fused_computation.44 | convolution fusion | flops 566498304 | bytes 68190208 | tf_op jit(solution)/shard_map/hqk,khd->qhd/dot_general | solution.py:289
  403.6 24.1 %fusion.40 = bf16[1024,1,4,64]{0,3,2,1:T(8,128)(2,1)} fusion(f32[4,1024,1024]{1,2,0:T(8,128)} %fusion.58, f32[4,1024,1024]{1,2,0:T(8,128)} %get-tuple-element.148, f32[4,1024]{1,0:T(4,128)S(1)} %log_add_fusion, bf16[1024,3,4,64]{0,3,2,1:T(8,128)(2,1)} %bitcast.170), kind=kOutput, calls=%fused_computation.43 | convolution fusion | flops 566498304 | bytes 68190208 | tf_op jit(solution)/shard_map/hqk,qhd->khd/dot_general | solution.py:290
  427.8 8.8 %fusion.37 = bf16[1024,1,4,64]{0,3,2,1:T(8,128)(2,1)S(1)} fusion(bf16[1024,4,64]{0,2,1:T(8,128)(2,1)} %bitcast.162, f32[4,1024,1024]{1,2,0:T(8,128)} %get-tuple-element.148, f32[4,1024]{1,0:T(4,128)S(1)} %log_add_fusion), kind=kOutput, calls=%fused_computation.42 | convolution fusion | flops 545521664 | bytes 17842176 | tf_op jit(solution)/shard_map/hqk,qhd->khd/dot_general | solution.py:285
  438.0 5.9 fusion.64
  445.9 7.6 %fusion.83 = f32[800,1600]{0,1:T(8,128)} fusion(bf16[1024,800]{1,0:T(8,128)(2,1)} %copy-done.40, bf16[1024,1600]{1,0:T(8,128)(2,1)S(1)} %copy-done.6), kind=kOutput, calls=%fused_computation.143 | convolution fusion | flops 2621440000 | bytes 10035200 | tf_op jit(solution)/shard_map/dot_general | solution.py:243
  454.7 4.6 fusion.81
  463.3 34.5 %plane_reduce_6.1 = f32[128,1600]{1,0:T(8,128)S(1)} custom-call(bf16[1024,768]{1,0:T(8,128)(2,1)S(1)} %copy.229.lhs_ref, bf16[1600,768]{1,0:T(8,128)(2,1)S(1)} %copy-done.11), custom_call_target="tpu_custom_call" | custom-call | flops 2516582400 | bytes 62914560 | tf_op jit(solution)/shard_map/plane_reduce_6/pallas_call | solution.py:220
  498.3 2.6 all_to_all.47
  500.9 3.6 all-to-all-start.2
  504.5 2.4 fusion.54
  506.9 29.0 %reduce-scatter.8.cloned.1.call-done = f32[400,768]{1,0:T(8,128)} async-done(((f32[1600,768]{1,0:T(8,128)}), f32[400,768]{1,0:T(8,128)}) %reduce-scatter.8.cloned.1.call-update) | async-done | bytes 1228816 | tf_op jit(solution)/shard_map/reduce_scatter | solution.py:380
  538.2 3.6 all-to-all-start
  541.8 98.7 %reduce-scatter.14.cloned.1.call-done = f32[800,400]{0,1:T(8,128)} async-done(((f32[800,1600]{0,1:T(8,128)}), f32[800,400]{0,1:T(8,128)}) %reduce-scatter.14.cloned.1.call-update) | async-done | bytes 1280016 | tf_op jit(solution)/shard_map/reduce_scatter | solution.py:380
  640.5 2.6 all_to_all.51
  643.1 4.3 all-to-all-start.3
  648.7 2.4 all_gather.39
  652.4 47.3 %psum.7 = f32[4,1600]{1,0:T(4,128)S(1)} all-reduce(f32[4,1600]{1,0:T(4,128)S(1)} %pad_maximum_fusion.2), channel_id=1, replica_groups=mesh['fsdp'=4,'ctx'=4,'tp'=2] {'fsdp','ctx','tp'}, use_global_device_ids=true, to_apply=%region_18.19 | all-reduce | flops 6400 | bytes 51200 | tf_op jit(solution)/shard_map/psum | solution.py:412
  701.5 3.7 all-to-all-start.1
  707.3 2.9 all_to_all.50
  713.7 2.6 copy.250
  723.9 3.2 concatenate.14
  727.1 2.6 convert_element_type.83
  (190 shorter events, 57.2 us)
Async XLA Ops:
  7.2 33.5 %copy-start = (bf16[400,3200]{1,0:T(8,128)(2,1)S(1)}, bf16[400,3200]{1,0:T(8,128)(2,1)}, u32[]{:S(2)}) copy-start(bf16[400,3200]{1,0:T(8,128)(2,1)} %param.19) | copy-start | bytes 7680004
  7.2 113.5 %all-gather.10.cloned.1.call-start = ((), (), s32[]{:S(2)}) async-start(), calls=%async_computation.9 | async-start | bytes 3072000 | tf_op jit(solution)/shard_map/all_gather | solution.py:319
  9.8 155.0 %all-gather.12.cloned.1.call-start = ((), (), s32[]{:S(2)}) async-start(), calls=%async_computation.10 | async-start | bytes 5990400 | tf_op jit(solution)/shard_map/all_gather | solution.py:322
  10.9 33.4 %copy-start.36 = (s32[1,256]{1,0:T(1,128)S(1)}, s32[1,256]{1,0:T(1,128)}, u32[]{:S(2)}) copy-start(s32[1,256]{1,0:T(1,128)} %param.12) | copy-start | bytes 3076
  40.6 11.7 %copy-start.24 = (bf16[1,256,1600]{1,2,0:T(8,128)(2,1)S(1)}, bf16[1,256,1600]{1,2,0:T(8,128)(2,1)}, u32[]{:S(2)}) copy-start(bf16[1,256,1600]{1,2,0:T(8,128)(2,1)} %param.11) | copy-start | bytes 2457604
  40.6 152.4 %all-gather.14.cloned.1.call-start = ((), (), s32[]{:S(2)}) async-start(), calls=%async_computation.11 | async-start | bytes 3584000 | tf_op jit(solution)/shard_map/all_gather | solution.py:324
  41.8 11.5 %copy-start.25 = (bf16[1,256,1600]{1,2,0:T(8,128)(2,1)S(1)}, bf16[1,256,1600]{1,2,0:T(8,128)(2,1)}, u32[]{:S(2)}) copy-start(bf16[1,256,1600]{1,2,0:T(8,128)(2,1)} %param.21) | copy-start | bytes 2457604
  41.8 201.4 %all-gather.16.cloned.1.call-start = ((), (), s32[]{:S(2)}) async-start(), calls=%async_computation.12 | async-start | bytes 3584000 | tf_op jit(solution)/shard_map/all_gather | solution.py:325
  44.3 296.3 %reduce-scatter.6.cloned.1.call-start = ((), (), s32[]{:S(2)}) async-start(), calls=%async_computation.13 | async-start | bytes 7667712 | tf_op jit(solution)/shard_map/reduce_scatter | solution.py:357
  79.1 1.7 copy-start.4
  79.6 41.1 %copy-start.29 = (f32[1600]{0:T(1024)S(1)}, f32[1600]{0:T(1024)}, u32[]{:S(2)}) copy-start(f32[1600]{0:T(1024)} %param.13) | copy-start | bytes 19204
  79.6 41.1 %copy-start.38 = (f32[1600]{0:T(1024)S(1)}, f32[1600]{0:T(1024)}, u32[]{:S(2)}) copy-start(f32[1600]{0:T(1024)} %param.14) | copy-start | bytes 19204
  79.6 46.3 %copy-start.31 = (f32[1024]{0:T(1024)}, f32[1024]{0:T(1024)S(1)}, u32[]{:S(2)}) copy-start(f32[1024]{0:T(1024)S(1)} %broadcast_multiply_fusion) | copy-start | bytes 12292
  80.7 45.3 %copy-start.34 = (f32[1024]{0:T(1024)}, f32[1024]{0:T(1024)S(1)}, u32[]{:S(2)}) copy-start(f32[1024]{0:T(1024)S(1)} %add_rsqrt_fusion) | copy-start | bytes 12292
  118.9 1.7 copy-start.5
  120.7 5.3 copy-start.19
  126.0 15.8 %copy-start.22 = (bf16[1024,768]{0,1:T(8,128)(2,1)}, bf16[1024,768]{0,1:T(8,128)(2,1)S(1)}, u32[]{:S(2)}) copy-start(bf16[1024,768]{0,1:T(8,128)(2,1)S(1)} %convolution_convert_fusion) | copy-start | bytes 4718596
  141.8 8.3 %copy-start.27 = (f32[4,1024]{1,0:T(4,128)}, f32[4,1024]{1,0:T(4,128)S(1)}, u32[]{:S(2)}) copy-start(f32[4,1024]{1,0:T(4,128)S(1)} %fusion.4) | copy-start | bytes 49156
  164.7 4.8 copy-start.26
  164.7 4.8 copy-start.33
  191.3 1.7 copy-start.7
  243.3 13.2 %copy-start.37 = (bf16[800,1600]{0,1:T(8,128)(2,1)S(1)}, bf16[800,1600]{0,1:T(8,128)(2,1)}, u32[]{:S(2)}) copy-start(bf16[800,1600]{0,1:T(8,128)(2,1)} %all-gather.16.cloned.1.call-done) | copy-start | bytes 7680004
  255.2 1.2 copy-start.40
  262.5 235.8 %reduce-scatter.12.cloned.1.call-start = ((), (), s32[]{:S(2)}) async-start(), calls=%async_computation.17 | async-start | bytes 7168000 | tf_op jit(solution)/shard_map/reduce_scatter | solution.py:380
  271.8 264.1 %reduce-scatter.8.cloned.1.call-start = ((), (), s32[]{:S(2)}) async-start(), calls=%async_computation.15 | async-start | bytes 6144000 | tf_op jit(solution)/shard_map/reduce_scatter | solution.py:380
  272.6 2.3 copy-start.10
  274.8 1.7 copy-start.12
  276.5 54.4 %copy-start.14 = (f32[128,1600]{1,0:T(8,128)S(1)}, f32[128,1600]{1,0:T(8,128)}, u32[]{:S(2)}) copy-start(f32[128,1600]{1,0:T(8,128)} %copy-done.13) | copy-start | bytes 2457604
  367.6 4.3 copy-start.23
  427.7 8.9 %copy-start.20 = (bf16[1024,1,4,64]{0,3,2,1:T(8,128)(2,1)S(1)}, bf16[1024,1,4,64]{0,3,2,1:T(8,128)(2,1)}, u32[]{:S(2)}) copy-start(bf16[1024,1,4,64]{0,3,2,1:T(8,128)(2,1)} %fusion.43) | copy-start | bytes 1572868
  427.8 8.9 %copy-start.21 = (bf16[1024,1,4,64]{0,3,2,1:T(8,128)(2,1)S(1)}, bf16[1024,1,4,64]{0,3,2,1:T(8,128)(2,1)}, u32[]{:S(2)}) copy-start(bf16[1024,1,4,64]{0,3,2,1:T(8,128)(2,1)} %fusion.40) | copy-start | bytes 1572868
  427.8 10.2 %copy-start.30 = (f32[1600]{0:T(1024)S(1)}, f32[1600]{0:T(1024)}, u32[]{:S(2)}) copy-start(f32[1600]{0:T(1024)} %param.13) | copy-start | bytes 19204
  427.8 10.2 %copy-start.32 = (f32[1024]{0:T(1024)S(1)}, f32[1024]{0:T(1024)}, u32[]{:S(2)}) copy-start(f32[1024]{0:T(1024)} %copy-done.31) | copy-start | bytes 12292
  427.8 10.2 %copy-start.35 = (f32[1024]{0:T(1024)S(1)}, f32[1024]{0:T(1024)}, u32[]{:S(2)}) copy-start(f32[1024]{0:T(1024)} %copy-done.34) | copy-start | bytes 12292
  427.8 10.2 %copy-start.39 = (f32[1600]{0:T(1024)S(1)}, f32[1600]{0:T(1024)}, u32[]{:S(2)}) copy-start(f32[1600]{0:T(1024)} %param.14) | copy-start | bytes 19204
  443.9 2.0 copy-start.6
  443.9 196.6 %reduce-scatter.14.cloned.1.call-start = ((), (), s32[]{:S(2)}) async-start(), calls=%async_computation.18 | async-start | bytes 7168000 | tf_op jit(solution)/shard_map/reduce_scatter | solution.py:380
  453.5 5.7 copy-start.3
  453.5 246.2 %reduce-scatter.10.cloned.1.call-start = ((), (), s32[]{:S(2)}) async-start(), calls=%async_computation.16 | async-start | bytes 2048000 | tf_op jit(solution)/shard_map/reduce_scatter | solution.py:380
  461.6 1.7 copy-start.11
  500.9 37.3 %all-to-all-start.2 = ((f32[4,100,800]{2,1,0:T(8,128)}), f32[4,100,800]{2,1,0:T(8,128)S(1)}, u32[]{:S(2)}, u32[]{:S(2)}) async-start(f32[4,100,800]{2,1,0:T(8,128)} %all_to_all.47), calls=%async_computation.6 | async-start | bytes 2981888 | tf_op jit(solution)/shard_map/all_to_all | solution.py:382
  504.4 209.3 %all-gather.18.cloned.1.call-start = ((), (), s32[]{:S(2)}) async-start(), calls=%async_computation.14 | async-start | bytes 2555904 | tf_op jit(solution)/shard_map/all_gather | solution.py:377
  538.2 104.9 %all-to-all-start = ((bf16[4,100,768]{2,1,0:T(8,128)(2,1)}), bf16[4,100,768]{2,1,0:T(8,128)(2,1)S(1)}, u32[]{:S(2)}, u32[]{:S(2)}) async-start(bf16[4,100,768]{2,1,0:T(8,128)(2,1)} %reshape.170), calls=%async_computation.2 | async-start | bytes 1277952 | tf_op jit(solution)/shard_map/all_to_all | solution.py:386
  541.8 106.8 %copy-start.18 = (bf16[128,1600]{1,0:T(8,128)(2,1)S(1)}, bf16[128,1600]{1,0:T(8,128)(2,1)}, u32[]{:S(2)}) copy-start(bf16[128,1600]{1,0:T(8,128)(2,1)} %get-tuple-element.103) | copy-start | bytes 1228804
  643.1 58.4 %all-to-all-start.3 = ((f32[800,4,100]{0,2,1:T(8,128)}), f32[800,4,100]{0,2,1:T(8,128)}, u32[]{:S(2)}, u32[]{:S(2)}) async-start(f32[800,4,100]{0,2,1:T(8,128)} %all_to_all.51), calls=%async_computation.8 | async-start | bytes 2981888 | tf_op jit(solution)/shard_map/all_to_all | solution.py:383
  647.5 73.1 %all-gather.20.cloned.1.call-start = ((), (), s32[]{:S(2)}) async-start(), calls=%async_computation.19 | async-start | bytes 1843200 | tf_op jit(solution)/shard_map/all_gather | solution.py:386
  701.5 14.8 %all-to-all-start.1 = ((bf16[256,4,100]{0,2,1:T(8,128)(2,1)}), bf16[256,4,100]{0,2,1:T(8,128)(2,1)S(1)}, u32[]{:S(2)}, u32[]{:S(2)}) async-start(bf16[256,4,100]{0,2,1:T(8,128)(2,1)} %all_to_all.44), calls=%async_computation.4 | async-start | bytes 425984 | tf_op jit(solution)/shard_map/all_to_all | solution.py:397
  722.5 7.3 copy-start.1
  (8 other events, 7.7 us)
Sparse Core Ops, SparseCore 0:
  10.1 60.6 all-gather.9
  73.3 50.1 all-gather.11
  125.7 57.9 all-gather.13
  185.7 57.5 all-gather.15
  262.6 77.9 reduce-scatter.5
  342.8 101.7 reduce-scatter.11
  446.9 88.9 reduce-scatter.7
  538.2 102.2 reduce-scatter.13
  643.4 37.1 reduce-scatter.9
  682.0 9.1 all-gather.17
  692.7 10.4 all-gather.19

commit v3 on v2

v3 whole, which is shorter than its diff:
```python
import functools

import jax
import jax.numpy as jnp
from jax import lax
from jax.experimental import pallas as pl
from jax.experimental.pallas import tpu as pltpu
from jax.sharding import PartitionSpec as P


H = 25
HD = 64
EPS = 1e-05
BF = jnp.bfloat16
F32 = jnp.float32
HALF_FLOAT = jnp.float16


VMEM = pl.BlockSpec(memory_space=pltpu.VMEM)
MESH = pl.DeviceIdType.MESH


def flip(index, stride):
    return index + stride * (1 - 2 * ((index // stride) % 2))


def strides_of(ctx_n, tp_i):
    bits = ctx_n.bit_length() - 1
    plain = [1 << b for b in range(bits)]
    turned = plain[1:] + plain[:1]
    return [a + (b - a) * tp_i for a, b in zip(plain, turned)]


def greet(partners):
    barrier = pltpu.get_barrier_semaphore()
    for who in partners:
        pl.semaphore_signal(barrier, inc=1, device_id=who, device_id_type=MESH)
    pl.semaphore_wait(barrier, len(partners))


def remote(src, dst, send, recv, who):
    return pltpu.make_async_remote_copy(
        src_ref=src, dst_ref=dst, send_sem=send, recv_sem=recv, device_id=who, device_id_type=MESH
    )


def comm_params(ident, limit):
    return pltpu.CompilerParams(
        collective_id=ident, has_side_effects=True, vmem_limit_bytes=limit
    )


def gather_kernel(ctx_n, tp_n, count, *refs):
    owns, alls = refs[:count], refs[count : 2 * count]
    send, recv, sib_send, sib_recv, local_sem = refs[2 * count :]
    ctx_i, tp_i = lax.axis_index("ctx"), lax.axis_index("tp")
    strides = strides_of(ctx_n, tp_i)
    sibling = {"tp": 1 - tp_i}
    greet([{"ctx": flip(ctx_i, s)} for s in strides] + [sibling])
    pending = []

    def place(n, c):
        rows = owns[n].shape[0]
        return alls[n].at[pl.ds(pl.multiple_of((c * tp_n + tp_i) * rows, rows), rows)]

    def pass_on(n, source, c, which):
        copy = remote(source, place(n, c), sib_send.at[n, which], sib_recv.at[n, which], sibling)
        copy.start()
        pending.append(copy)

    mine = [pltpu.make_async_copy(owns[n], place(n, ctx_i), local_sem.at[n]) for n in range(count)]
    held, slot = [ctx_i], 0
    for stride in strides:
        partner = {"ctx": flip(ctx_i, stride)}
        copies = []
        for position, c in enumerate(held):
            for n in range(count):
                source = owns[n] if position == 0 else place(n, c)
                copy = remote(source, place(n, c), send.at[n, slot], recv.at[n, slot], partner)
                copy.start()
                copies.append((copy, n, slot + 1, flip(c, stride)))
            slot += 1
        if len(held) == 1:
            for n in range(count):
                mine[n].start()
                pass_on(n, owns[n], ctx_i, 0)
        for copy, n, which, fresh in copies:
            copy.wait_recv()
            pass_on(n, place(n, fresh), fresh, which)
        for copy, _, _, _ in copies:
            copy.wait_send()
        held = held + [flip(c, stride) for c in held]
    for copy in pending + mine:
        copy.wait()


def plane_gather(owns, ctx_n, tp_n, ident):
    count = len(owns)
    return pl.pallas_call(
        functools.partial(gather_kernel, ctx_n, tp_n, count),
        out_shape=tuple(
            jax.ShapeDtypeStruct((own.shape[0] * ctx_n * tp_n, own.shape[1]), own.dtype)
            for own in owns
        ),
        in_specs=[VMEM] * count,
        out_specs=(VMEM,) * count,
        scratch_shapes=[
            pltpu.SemaphoreType.DMA((count, ctx_n - 1)),
            pltpu.SemaphoreType.DMA((count, ctx_n - 1)),
            pltpu.SemaphoreType.DMA((count, ctx_n)),
            pltpu.SemaphoreType.DMA((count, ctx_n)),
            pltpu.SemaphoreType.DMA((count,)),
        ],
        compiler_params=comm_params(ident, 24 << 20),
        cost_estimate=pl.CostEstimate(flops=0, bytes_accessed=30 << 20, transcendentals=0),
    )(*owns)


def sum_kernel(mesh_shape, tiles_ref, out_ref, got, send, recv):
    fsdp_n, ctx_n, tp_n = mesh_shape
    total = fsdp_n * ctx_n * tp_n
    me = (lax.axis_index("fsdp") * ctx_n + lax.axis_index("ctx")) * tp_n + lax.axis_index("tp")
    others = [lax.rem(me + shift, total) for shift in range(1, total)]
    ids = [
        {"fsdp": o // (ctx_n * tp_n), "ctx": (o // tp_n) % ctx_n, "tp": o % tp_n} for o in others
    ]
    greet(ids)
    copies = []
    for i, (other, who) in enumerate(zip(others, ids)):
        copy = remote(tiles_ref.at[other // tp_n], got.at[i], send.at[i], recv.at[i], who)
        copy.start()
        copies.append(copy)
    value = tiles_ref[me // tp_n]
    for i, copy in enumerate(copies):
        copy.wait_recv()
        value = value + got[i]
    out_ref[...] = value
    for copy in copies:
        copy.wait_send()


def sum_everywhere(rows, mesh_shape, ident):
    fsdp_n, ctx_n, tp_n = mesh_shape
    places = fsdp_n * ctx_n
    share = rows.shape[1] // places
    tiles = jnp.transpose(rows.reshape(rows.shape[0], places, share), (1, 0, 2))
    tiles = jnp.pad(tiles, ((0, 0), (0, 8 - rows.shape[0]), (0, 128 - share)))
    total = pl.pallas_call(
        functools.partial(sum_kernel, mesh_shape),
        out_shape=jax.ShapeDtypeStruct((8, 128), F32),
        in_specs=[VMEM],
        out_specs=VMEM,
        scratch_shapes=[
            pltpu.VMEM((places * tp_n - 1, 8, 128), F32),
            pltpu.SemaphoreType.DMA((places * tp_n - 1,)),
            pltpu.SemaphoreType.DMA((places * tp_n - 1,)),
        ],
        compiler_params=comm_params(ident, 8 << 20),
        cost_estimate=pl.CostEstimate(flops=0, bytes_accessed=15 << 20, transcendentals=0),
        name="sum_everywhere",
    )(tiles)
    return total[: rows.shape[0], :share]


def reduce_kernel(
    ctx_n, tp_n, turned, lhs_ref, rhs_ref, out_ref,
    part, near, got, sib_send, sib_recv, send, recv,
):
    rows = out_ref.shape[0]
    ctx_i, tp_i = lax.axis_index("ctx"), lax.axis_index("tp")
    strides = strides_of(ctx_n, tp_i)
    sibling = {"tp": 1 - tp_i}
    greet([{"ctx": flip(ctx_i, s)} for s in strides] + [sibling])
    contract = ((1,), (1,)) if turned else ((1,), (0,))
    to_sibling, onward = {}, {}
    bits = len(strides)

    def common(r):
        turn = sum(1 << ((b + 1) % bits) for b in range(bits) if r >> b & 1)
        return r + (turn - r) * tp_i

    def first(r):
        c = ctx_i
        for b, stride in enumerate(strides):
            if r >> b & 1:
                c = flip(c, stride)
        pair = lhs_ref[pl.ds(pl.multiple_of(c * tp_n * rows, tp_n * rows), tp_n * rows), :]
        part[r] = dot(pair, rhs_ref[...], contract).reshape(tp_n, rows, rhs_ref.shape[0 if turned else 1])
        to_sibling[r] = remote(
            part.at[r, 1 - tp_i], near.at[common(r)],
            sib_send.at[r], sib_recv.at[common(r)], sibling,
        )
        to_sibling[r].start()

    def second(r):
        to_sibling[r].wait_recv()
        total = part[r, tp_i] + near[common(r)]
        high = r.bit_length() - 1
        for b in range(high + 1, len(strides)):
            slot = (1 << b) - 1 + r
            onward[(1 << b) + r].wait_recv()
            total = total + got[slot]
        if r:
            near[common(r)] = total
            slot = r - 1
            onward[r] = remote(
                near.at[common(r)], got.at[slot], send.at[slot], recv.at[slot],
                {"ctx": flip(ctx_i, strides[high])},
            )
            onward[r].start()
        else:
            out_ref[...] = total

    order = list(range(ctx_n - 1, -1, -1))
    for i, r in enumerate(order):
        first(r)
        if i:
            second(order[i - 1])
    second(order[-1])
    for copy in list(to_sibling.values()) + list(onward.values()):
        copy.wait_send()


def plane_reduce(lhs, rhs, ctx_n, tp_n, turned, ident):
    members = ctx_n * tp_n
    rows = lhs.shape[0] // members
    columns = rhs.shape[0 if turned else 1]
    inner = lhs.shape[1]
    return pl.pallas_call(
        functools.partial(reduce_kernel, ctx_n, tp_n, turned),
        out_shape=jax.ShapeDtypeStruct((rows, columns), F32),
        in_specs=[VMEM, VMEM],
        out_specs=VMEM,
        scratch_shapes=[
            pltpu.VMEM((ctx_n, tp_n, rows, columns), F32),
            pltpu.VMEM((ctx_n, rows, columns), F32),
            pltpu.VMEM((ctx_n - 1, rows, columns), F32),
            pltpu.SemaphoreType.DMA((ctx_n,)),
            pltpu.SemaphoreType.DMA((ctx_n,)),
            pltpu.SemaphoreType.DMA((ctx_n - 1,)),
            pltpu.SemaphoreType.DMA((ctx_n - 1,)),
        ],
        compiler_params=comm_params(ident, 48 << 20),
        cost_estimate=pl.CostEstimate(
            flops=2 * lhs.shape[0] * inner * columns, bytes_accessed=60 << 20, transcendentals=0
        ),
    )(lhs, rhs)


def dot(lhs, rhs, dims):
    return lax.dot_general(lhs, rhs, (dims, ((), ())), preferred_element_type=F32)


def moments(values):
    centered = values - jnp.mean(values, axis=-1, keepdims=True)
    inv_std = lax.rsqrt(jnp.mean(centered * centered, axis=-1, keepdims=True) + EPS)
    return centered * inv_std, inv_std


def norm_back(upstream, normed, inv_std, gain):
    scaled = upstream * gain
    return inv_std * (
        scaled
        - jnp.mean(scaled, axis=-1, keepdims=True)
        - normed * jnp.mean(scaled * normed, axis=-1, keepdims=True)
    )


HALF = 2 * HD


def mask_bias(seg_row_ref, seg_col_ref, i, j, block):
    same = seg_col_ref[pl.ds(j * block, block), :] == seg_row_ref[:, pl.ds(i * block, block)]
    if i == j:
        key = lax.broadcasted_iota(jnp.int32, (block, block), 0)
        query = lax.broadcasted_iota(jnp.int32, (block, block), 1)
        same = same & (key <= query)
    return same


def attend_kernel(block, q_ref, k_ref, v_ref, row_ref, col_ref, out_ref, lse_ref, qt, vt, ot, s_ref):
    length = q_ref.shape[0]
    qt[...] = q_ref[...].T
    vt[...] = v_ref[...].T
    for h in range(2):
        head = slice(h * HD, (h + 1) * HD)
        for i in range(length // block):
            cols = slice(i * block, (i + 1) * block)
            row_max = None
            for j in range(i + 1):
                s = dot(k_ref[j * block : (j + 1) * block, head], qt[head, cols], ((1,), (0,)))
                s = jnp.where(mask_bias(row_ref, col_ref, i, j, block), s * HD ** (-0.5), -1e30)
                s_ref[j * block : (j + 1) * block, :] = s
                top = jnp.max(s, axis=0, keepdims=True)
                row_max = top if row_max is None else jnp.maximum(row_max, top)
            total = jnp.zeros((1, block), F32)
            for j in range(i + 1):
                e = jnp.exp(s_ref[j * block : (j + 1) * block, :] - row_max)
                s_ref[j * block : (j + 1) * block, :] = e
                total = total + jnp.sum(e, axis=0, keepdims=True)
            scale = 1.0 / total
            acc = jnp.zeros((HD, block), F32)
            for j in range(i + 1):
                p = (s_ref[j * block : (j + 1) * block, :] * scale).astype(BF)
                acc = acc + dot(vt[head, j * block : (j + 1) * block], p, ((1,), (0,)))
            ot[head, cols] = acc
            lse_ref[0, h : h + 1, cols] = row_max + jnp.log(total)
    out_ref[...] = ot[...].T.astype(BF)


def attention(qkv, seg, slots):
    length = qkv.shape[0]
    pairs = slots // 2
    block = min(256, length)
    return pl.pallas_call(
        functools.partial(attend_kernel, block),
        grid=(pairs,),
        out_shape=(
            jax.ShapeDtypeStruct((length, slots * HD), BF),
            jax.ShapeDtypeStruct((pairs, 2, length), F32),
        ),
        in_specs=[
            pl.BlockSpec((length, HALF), lambda p: (0, p)),
            pl.BlockSpec((length, HALF), lambda p: (0, pairs + p)),
            pl.BlockSpec((length, HALF), lambda p: (0, 2 * pairs + p)),
            pl.BlockSpec((1, length), lambda p: (0, 0)),
            pl.BlockSpec((length, 1), lambda p: (0, 0)),
        ],
        out_specs=(
            pl.BlockSpec((length, HALF), lambda p: (0, p)),
            pl.BlockSpec((1, 2, length), lambda p: (p, 0, 0)),
        ),
        scratch_shapes=[
            pltpu.VMEM((HALF, length), BF),
            pltpu.VMEM((HALF, length), BF),
            pltpu.VMEM((HALF, length), F32),
            pltpu.VMEM((length, block), F32),
        ],
        compiler_params=pltpu.CompilerParams(vmem_limit_bytes=24 << 20),
        cost_estimate=pl.CostEstimate(
            flops=4 * length * length * slots * HD, bytes_accessed=40 << 20, transcendentals=0
        ),
        name="attend",
    )(qkv, qkv, qkv, seg[None, :], seg[:, None])


def attend_back_kernel(
    block, pairs, q_ref, k_ref, v_ref, g_ref, lse_ref, row_ref, col_ref, out_ref,
    qt, kt, gt, dqt, dkt, dvt, p_ref, dp_ref,
):
    length = q_ref.shape[0]
    scale = HD ** (-0.5)
    qt[...] = q_ref[...].T
    kt[...] = k_ref[...].T
    gt[...] = g_ref[...].T
    for h in range(2):
        head = slice(h * HD, (h + 1) * HD)
        for i in range(length // block):
            cols = slice(i * block, (i + 1) * block)
            lse = lse_ref[0, h : h + 1, cols]
            inner = jnp.zeros((1, block), F32)
            for j in range(i + 1):
                keys = slice(j * block, (j + 1) * block)
                s = dot(k_ref[keys, head], qt[head, cols], ((1,), (0,))) * scale
                s = jnp.where(mask_bias(row_ref, col_ref, i, j, block), s, -1e30)
                p = jnp.exp(s - lse)
                dp = dot(v_ref[keys, head], gt[head, cols], ((1,), (0,)))
                inner = inner + jnp.sum(p * dp, axis=0, keepdims=True)
                p_ref[keys, :] = p
                dp_ref[keys, :] = dp
                dv = dot(gt[head, cols], p.astype(BF), ((1,), (1,)))
                dvt[head, keys] = dv if i == j else dvt[head, keys] + dv
            acc = jnp.zeros((HD, block), F32)
            for j in range(i + 1):
                keys = slice(j * block, (j + 1) * block)
                ds = (p_ref[keys, :] * (dp_ref[keys, :] - inner) * scale).astype(BF)
                acc = acc + dot(kt[head, keys], ds, ((1,), (0,)))
                dk = dot(qt[head, cols], ds, ((1,), (1,)))
                dkt[head, keys] = dk if i == j else dkt[head, keys] + dk
            dqt[head, cols] = acc
    pair = pl.program_id(0)
    for part, ref in enumerate((dqt, dkt, dvt)):
        start = pl.multiple_of((part * pairs + pair) * HALF, HALF)
        out_ref[:, pl.ds(start, HALF)] = ref[...].T.astype(BF)


def attention_back(qkv, grad, lse, seg, slots):
    length = qkv.shape[0]
    pairs = slots // 2
    block = min(256, length)
    return pl.pallas_call(
        functools.partial(attend_back_kernel, block, pairs),
        grid=(pairs,),
        out_shape=jax.ShapeDtypeStruct((length, 3 * slots * HD), BF),
        in_specs=[
            pl.BlockSpec((length, HALF), lambda p: (0, p)),
            pl.BlockSpec((length, HALF), lambda p: (0, pairs + p)),
            pl.BlockSpec((length, HALF), lambda p: (0, 2 * pairs + p)),
            pl.BlockSpec((length, HALF), lambda p: (0, p)),
            pl.BlockSpec((1, 2, length), lambda p: (p, 0, 0)),
            pl.BlockSpec((1, length), lambda p: (0, 0)),
            pl.BlockSpec((length, 1), lambda p: (0, 0)),
        ],
        out_specs=pl.BlockSpec((length, 3 * slots * HD), lambda p: (0, 0)),
        scratch_shapes=[
            pltpu.VMEM((HALF, length), BF),
            pltpu.VMEM((HALF, length), BF),
            pltpu.VMEM((HALF, length), BF),
            pltpu.VMEM((HALF, length), F32),
            pltpu.VMEM((HALF, length), F32),
            pltpu.VMEM((HALF, length), F32),
            pltpu.VMEM((length, block), F32),
            pltpu.VMEM((length, block), F32),
        ],
        compiler_params=pltpu.CompilerParams(vmem_limit_bytes=32 << 20),
        cost_estimate=pl.CostEstimate(
            flops=10 * length * length * slots * HD, bytes_accessed=80 << 20, transcendentals=0
        ),
        name="attend_back",
    )(qkv, qkv, qkv, grad, lse, seg[None, :], seg[:, None])


def weight_grad_kernel(fsdp_n, lhs_ref, rhs_ref, own_ref, *refs):
    sent, full = refs[: fsdp_n - 1], refs[fsdp_n - 1]
    rows, columns = own_ref.shape
    me = lax.axis_index("fsdp")
    tops = []
    step = rows if rows % 128 else 4 * 128
    for r in range(0, full.shape[0], step):
        part = slice(r, min(r + step, full.shape[0]))
        value = dot(lhs_ref[:, part], rhs_ref[...], ((0,), (0,)))
        full[part, :] = value
        tops.append(jnp.max(jnp.abs(value)))
    top = jnp.full((1, columns), functools.reduce(jnp.maximum, tops))
    exponent = jnp.floor(jnp.log2(jnp.maximum(top, 1e-30)))
    scale = jnp.exp2(14.0 - exponent)

    def block(index):
        return full[pl.ds(pl.multiple_of(index * rows, rows), rows), :]

    own_ref[...] = block(me)
    for s, ref in enumerate(sent, 1):
        ref[:rows, :] = block(lax.rem(me + s, fsdp_n)) * scale
        ref[rows:, :] = jnp.broadcast_to(exponent, (ref.shape[0] - rows, columns))


def weight_grad(lhs, rhs, fsdp_n):
    rows, columns = lhs.shape[1] // fsdp_n, rhs.shape[1]
    blocks = pl.pallas_call(
        functools.partial(weight_grad_kernel, fsdp_n),
        out_shape=(jax.ShapeDtypeStruct((rows, columns), F32),)
        + (jax.ShapeDtypeStruct((rows + 16, columns), F32),) * (fsdp_n - 1),
        in_specs=[VMEM, VMEM],
        out_specs=(VMEM,) * fsdp_n,
        scratch_shapes=[pltpu.VMEM((lhs.shape[1], columns), F32)],
        compiler_params=pltpu.CompilerParams(vmem_limit_bytes=30 << 20),
        cost_estimate=pl.CostEstimate(
            flops=2 * lhs.shape[0] * lhs.shape[1] * columns,
            bytes_accessed=20 << 20,
            transcendentals=0,
        ),
        name="weight_grad",
    )(lhs, rhs)
    arrived = {}
    for shift in sorted(range(1, fsdp_n), key=lambda v: min(v, fsdp_n - v)):
        arrived[shift] = lax.ppermute(
            blocks[shift].astype(HALF_FLOAT),
            "fsdp",
            [(i, (i + shift) % fsdp_n) for i in range(fsdp_n)],
        )

    def finish(dtype=F32):
        total = blocks[0]
        for block_in in arrived.values():
            back = jnp.exp2(block_in[rows, 0].astype(F32) - 14.0)
            total = total + block_in[:rows].astype(F32) * back
        return total.astype(dtype)

    return finish


GELU_A = (2.0 / jnp.pi) ** 0.5
GELU_B = 0.044715


def activate_kernel(h_ref, w_ref, pre_ref, act_ref):
    u = dot(h_ref[...], w_ref[...], ((1,), (0,)))
    pre_ref[...] = u
    act_ref[...] = (0.5 * u * (1.0 + jnp.tanh(GELU_A * (u + GELU_B * (u * u * u))))).astype(BF)


def activate_back_kernel(g_ref, w_ref, pre_ref, out_ref):
    upstream = dot(g_ref[...], w_ref[...], ((1,), (0,)))
    u = pre_ref[...]
    t = jnp.tanh(GELU_A * (u + GELU_B * (u * u * u)))
    slope = 0.5 * (1.0 + t) + 0.5 * u * (1.0 - t * t) * (GELU_A * (1.0 + 3.0 * GELU_B * (u * u)))
    out_ref[...] = (upstream * slope).astype(BF)


def row_blocks(kernel, lhs, rhs, others, out_dtypes):
    length, inner = lhs.shape
    columns = rhs.shape[1]
    block = min(256, length)
    wide = pl.BlockSpec((block, columns), lambda i: (i, 0))
    return pl.pallas_call(
        kernel,
        grid=(length // block,),
        out_shape=tuple(jax.ShapeDtypeStruct((length, columns), d) for d in out_dtypes),
        in_specs=[
            pl.BlockSpec((block, inner), lambda i: (i, 0)),
            pl.BlockSpec((inner, columns), lambda i: (0, 0)),
        ]
        + [wide] * len(others),
        out_specs=(wide,) * len(out_dtypes),
        compiler_params=pltpu.CompilerParams(vmem_limit_bytes=24 << 20),
        cost_estimate=pl.CostEstimate(
            flops=2 * length * inner * columns, bytes_accessed=20 << 20, transcendentals=0
        ),
    )(lhs, rhs, *others)


def place_kernel(ctx_n, tp_n, counts, src_ref, out_ref, got, send, recv, sib_send, sib_recv, local_sem):
    ctx_i, tp_i = lax.axis_index("ctx"), lax.axis_index("tp")
    sibling = {"tp": 1 - tp_i}
    others = [lax.rem(ctx_i + shift, ctx_n) for shift in range(1, ctx_n)]
    greet([{"ctx": c} for c in others] + [sibling])
    me = ctx_i * tp_n + tp_i
    copies = []
    for i, c in enumerate(others):
        copy = remote(src_ref.at[c], got.at[me], send.at[i], recv.at[i], {"ctx": c})
        copy.start()
        copies.append(copy)
    passed = [remote(src_ref.at[ctx_i], got.at[me], sib_send.at[0], sib_recv.at[0], sibling)]
    passed[0].start()
    mine = pltpu.make_async_copy(src_ref.at[ctx_i], got.at[me], local_sem)
    mine.start()
    for i, copy in enumerate(copies):
        copy.wait_recv()
        source = lax.rem(ctx_i + ctx_n - 1 - i, ctx_n) * tp_n + tp_i
        onward = remote(
            got.at[source], got.at[source], sib_send.at[i + 1], sib_recv.at[i + 1], sibling
        )
        onward.start()
        passed.append(onward)
    for copy in passed:
        copy.wait_recv()
    mine.wait()
    rows = out_ref.shape[0]
    width = src_ref.shape[2] // 3
    start = 0
    for p in range(3):
        for m, count in enumerate(counts):
            size = count * HD
            out_ref[:, start : start + size] = got[m, :rows, p * width : p * width + size].astype(F32)
            start += size
    for copy in copies + passed:
        copy.wait_send()


def place_heads(piece, ctx_n, tp_n, counts, ident):
    rows, columns = piece.shape[0] // ctx_n, piece.shape[1]
    members = ctx_n * tp_n
    tall = -(-rows // 16) * 16
    piece = jnp.pad(piece.reshape(ctx_n, rows, columns), ((0, 0), (0, tall - rows), (0, 0)))
    return pl.pallas_call(
        functools.partial(place_kernel, ctx_n, tp_n, counts),
        out_shape=jax.ShapeDtypeStruct((rows, 3 * sum(counts) * HD), F32),
        in_specs=[VMEM],
        out_specs=VMEM,
        scratch_shapes=[
            pltpu.VMEM((members, tall, columns), BF),
            pltpu.SemaphoreType.DMA((ctx_n - 1,)),
            pltpu.SemaphoreType.DMA((ctx_n - 1,)),
            pltpu.SemaphoreType.DMA((ctx_n,)),
            pltpu.SemaphoreType.DMA((ctx_n,)),
            pltpu.SemaphoreType.DMA,
        ],
        compiler_params=comm_params(ident, 16 << 20),
        cost_estimate=pl.CostEstimate(flops=0, bytes_accessed=20 << 20, transcendentals=0),
    )(piece)


def build(mesh):
    fsdp_n, ctx_n, tp_n = mesh.shape["fsdp"], mesh.shape["ctx"], mesh.shape["tp"]
    members = ctx_n * tp_n
    slots = 2 * -(-H // (2 * members))
    starts = [m * H // members for m in range(members + 1)]
    counts = [starts[m + 1] - starts[m] for m in range(members)]
    width = slots * HD

    def body(x, segments, g1, b1, wqkv, wout, g2, b2, wfc, wproj, cot):
        x, cot = x[0], cot[0]
        rows, model = x.shape
        tp_i, ctx_i = lax.axis_index("tp"), lax.axis_index("ctx")
        member = ctx_i * tp_n + tp_i
        own = rows // tp_n
        head0 = member * H // members
        head_n = (member + 1) * H // members - head0
        valid = jnp.arange(width, dtype=jnp.int32) < head_n * HD

        def cols(matrix, start, size):
            return lax.dynamic_slice_in_dim(matrix, start, size, 1)

        def rows_of(matrix, start, size):
            return lax.dynamic_slice_in_dim(matrix, start, size, 0)

        hidden = wfc.shape[1] // ctx_n
        wo = jnp.where(valid, rows_of(wout, head0 * HD, width).T, jnp.zeros((), BF))
        heads = [cols(wqkv, p * H * HD + head0 * HD, width) for p in range(3)]
        first = lax.all_gather(jnp.concatenate(heads + [wo], axis=1), "fsdp", axis=0, tiled=True)
        wq, wo = first[:, : 3 * width], first[:, 3 * width :]
        second = jnp.stack(
            [cols(wfc, ctx_i * hidden, hidden), rows_of(wproj, ctx_i * hidden, hidden).T]
        )
        second = lax.all_gather(second, "fsdp", axis=0)
        wf = second[:, 0].reshape(model, hidden)
        wp = second[:, 1].reshape(model, hidden)

        x_own = rows_of(x, tp_i * own, own)
        cot_own = rows_of(cot, tp_i * own, own)
        seg_own = jnp.broadcast_to(cols(segments, tp_i * own, own), (8, own))
        x_all, seg, cot_all = plane_gather((x_own, seg_own, cot_own), ctx_n, tp_n, 0)
        length = x_all.shape[0]
        seg = seg.reshape(members, 8, own)[:, 0].reshape(length)

        n1_all, _ = moments(x_all.astype(F32))
        h1 = (n1_all * g1 + b1).astype(BF)
        qkv = dot(h1, wq, ((1,), (0,))).astype(BF)
        attended, lse = attention(qkv, seg, slots)
        x_own_f32 = x_own.astype(F32)
        r1 = x_own_f32 + plane_reduce(attended, wo, ctx_n, tp_n, True, 1)
        n2, s2 = moments(r1)
        (h2,) = plane_gather(((n2 * g2 + b2).astype(BF),), ctx_n, tp_n, 2)
        pre, act = row_blocks(activate_kernel, h2, wf, (), (F32, BF))
        proj_sum = weight_grad(cot_all, act, fsdp_n)
        (grad_pre,) = row_blocks(activate_back_kernel, cot_all, wp, (pre,), (BF,))
        fc_sum = weight_grad(h2, grad_pre, fsdp_n)
        grad_h2 = plane_reduce(grad_pre, wf, ctx_n, tp_n, True, 3)
        grad_r1 = cot_own.astype(F32) + norm_back(grad_h2, n2, s2, g2)
        (grad_att,) = plane_gather((grad_r1.astype(BF),), ctx_n, tp_n, 4)
        out_sum = weight_grad(grad_att, attended, fsdp_n)
        grad_attended = dot(grad_att, wo, ((1,), (0,))).astype(BF)
        dqkv = attention_back(qkv, grad_attended, lse, seg, slots)
        qkv_sum = weight_grad(h1, dqkv, fsdp_n)
        late, _ = lax.optimization_barrier((act, dqkv))
        mlp = plane_reduce(late, wp, ctx_n, tp_n, True, 7)
        out = lax.all_gather((r1 + mlp).astype(BF), "tp", axis=0, tiled=True)
        grad_h1 = plane_reduce(dqkv, wq, ctx_n, tp_n, True, 5)
        n1, s1 = moments(x_own_f32)
        grad_x = grad_r1 + norm_back(grad_h1, n1, s1, g1)
        grad_x = lax.all_gather(grad_x, "tp", axis=0, tiled=True)

        def to_places(v):
            return lax.all_to_all(v.reshape(ctx_n, -1, v.shape[1]), "ctx", 0, 0, tiled=True)

        def side_by_side(v):
            return jnp.moveaxis(v, 0, 1).reshape(v.shape[1], -1)

        def of_members(v):
            v = lax.all_gather(to_places(v), "tp", axis=1)
            return v.reshape((members,) + v.shape[2:]).astype(F32)

        fc_out = side_by_side(to_places(fc_sum()))
        proj_out = side_by_side(to_places(proj_sum())).T
        go = of_members(out_sum(BF))
        out_out = jnp.concatenate(
            [go[m][:, : counts[m] * HD] for m in range(members)], axis=1
        ).T
        qkv_out = place_heads(qkv_sum(BF), ctx_n, tp_n, counts, 8)
        sums = jnp.stack(
            [
                jnp.sum(grad_h1 * n1, axis=0),
                jnp.sum(grad_h1, axis=0),
                jnp.sum(grad_h2 * n2, axis=0),
                jnp.sum(grad_h2, axis=0),
            ]
        )
        sums = sum_everywhere(sums, (fsdp_n, ctx_n, tp_n), 6)
        return (
            out[None],
            grad_x[None],
            sums[0],
            sums[1],
            qkv_out,
            out_out,
            sums[2],
            sums[3],
            fc_out,
            proj_out,
        )

    return body


def solution(mesh):
    placed = (
        P("fsdp", "ctx", None),
        P("fsdp", "ctx"),
        P(),
        P(),
        P("fsdp", None),
        P(None, "fsdp"),
        P(),
        P(),
        P("fsdp", "tp"),
        P("tp", "fsdp"),
        P("fsdp", "ctx", None),
    )
    both = ("fsdp", "ctx")
    return jax.shard_map(
        build(mesh),
        mesh=mesh,
        in_specs=placed,
        out_specs=(
            P("fsdp", "ctx", None),
            P("fsdp", "ctx", None),
            P(both),
            P(both),
            P(both, None),
            P(None, both),
            P(both),
            P(both),
            P(both, "tp"),
            P("tp", both),
        ),
        check_vma=False,
    )
```

time: 741 us -> 615 us (0.83)
  the two profiles are of different devices: /device:TPU:0 before, /device:TPU:9 now
where the time goes in v3:
time: 615 us; the launch traced here: 611 us
  Pallas kernels  288 us (47%)
  waiting for transfers between devices  165 us (27%)
  local copies, waits for them, and re-layouts  66.7 us (11%)
  other arithmetic  30.9 us (5%)
  starting transfers between devices  23.8 us (4%)
  between operations  23.3 us (4%)
  matrix products  8.48 us (1%)
    pallas_call x4, Pallas kernels, plane_reduce(): pl.pallas_call(functools.partial(reduce_kernel, ctx_n, tp_n, turned), out...  139 us
    ppermute x12, waiting for transfers between devices, weight_grad(): lax.ppermute(blocks[shift].astype(HALF_FLOAT), 'fsdp', [(i, (i + shift) %...  121 us
    pallas_call x3, Pallas kernels, plane_gather(): pl.pallas_call(functools.partial(gather_kernel, ctx_n, tp_n, count), out_...  79.6 us
    all_gather x1, waiting for transfers between devices, body(): second = lax.all_gather(second, 'fsdp', axis=0)  32.1 us
    unnamed x103, local copies, waits for them, and re-layouts  21.1 us
    pallas_call x4, Pallas kernels, weight_grad(): pl.pallas_call(functools.partial(weight_grad_kernel, fsdp_n), out_shape=(...  16.2 us
    pallas_call x1, Pallas kernels, place_heads(): pl.pallas_call(functools.partial(place_kernel, ctx_n, tp_n, counts), out_...  13.4 us
    ppermute x12, starting transfers between devices, weight_grad(): lax.ppermute(blocks[shift].astype(HALF_FLOAT), 'fsdp', [(i, (i + shift) %...  12.3 us
  transfers between devices with their start and end apart: 18, of which 5 were waited for; matrix products, arithmetic and copies ran while one was open for 12% of the time, Pallas kernels for 27%

profile of v3, /device:TPU:9, one launch (start us, length us, event | category | flops | bytes accessed | tf_op | source)
XLA Modules:
  0.0 611.4 jit_solution(13422845526970483450)
XLA Ops:
  11.4 1.5 dynamic-slice_bitcast_fusion.1
  18.4 36.5 %shard_map.186 = (bf16[1024,1600]{1,0:T(8,128)(2,1)S(1)}, s32[64,128]{1,0:T(8,128)S(1)}, bf16[1024,1600]{1,0:T(8,128)(2,1)S(1)}) custom-call(bf16[128,1600]{1,0:T(8,128)(2,1)S(1)} %bitcast.89, s32[8,128]{1,0:T(8,128)S(1)} %broadcast_in_dim.17.refs_1_, bf16[128,1600]{1,0:T(8,128)(2,1)S(1)} %bitcast.92), custom_call_target="tpu_custom_call" | custom-call | bytes 31457280 | tf_op jit(solution)/shard_map/pallas_call | solution.py:99
  54.9 1.8 copy-done.9
  60.5 2.9 fusion.5.lhs_ref
  63.4 12.0 %all-gather.6.cloned.1.call-done = bf16[1600,1024]{1,0:T(8,128)(2,1)} async-done(((bf16[400,1024]{1,0:T(8,128)(2,1)}), bf16[1600,1024]{1,0:T(8,128)(2,1)}) %all-gather.6.cloned.1.call-update) | async-done | bytes 3276816 | tf_op jit(solution)/shard_map/all_gather | solution.py:610
  76.6 5.8 convolution_convert_fusion.q_ref.k_ref.v_ref
  82.4 7.3 %attend.1 = (bf16[1024,256]{1,0:T(8,128)(2,1)S(1)}, f32[2,2,1024]{2,1,0:T(2,128)S(1)}) custom-call(bf16[1024,768]{1,0:T(8,128)(2,1)S(1)} %convolution_convert_fusion.q_ref.k_ref.v_ref, bf16[1024,768]{1,0:T(8,128)(2,1)S(1)} %convolution_convert_fusion.q_ref.k_ref.v_ref, bf16[1024,768]{1,0:T(8,128)(2,1)S(1)} %convolution_convert_fusion.q_ref.k_ref.v_ref, ...), custom_call_target="tpu_custom_call" | custom-call | flops 1073741824 | bytes 41943040 | tf_op jit(solution)/shard_map/attend/pallas_call | solution.py:315
  89.7 34.6 %shard_map.187 = f32[128,1600]{1,0:T(8,128)S(1)} custom-call(bf16[1024,256]{1,0:T(8,128)(2,1)S(1)} %get-tuple-element.36.lhs_ref.rhs_ref, bf16[1600,256]{1,0:T(8,128)(2,1)S(1)} %slice.199.rhs_ref), custom_call_target="tpu_custom_call" | custom-call | flops 838860800 | bytes 62914560 | tf_op jit(solution)/shard_map/pallas_call | solution.py:229
  125.8 21.6 %shard_map.188.h_ref.lhs_ref = bf16[1024,1600]{1,0:T(8,128)(2,1)S(1)} custom-call(bf16[128,1600]{1,0:T(8,128)(2,1)S(1)} %add_convert_fusion.2.refs_0_), custom_call_target="tpu_custom_call" | custom-call | bytes 31457280 | tf_op jit(solution)/shard_map/pallas_call | solution.py:99
  147.4 1.9 slice.197.rhs_ref
  149.9 32.1 %all-gather.10.cloned.1.call-done = bf16[8,400,800]{2,1,0:T(8,128)(2,1)} async-done(((bf16[2,400,800]{2,1,0:T(8,128)(2,1)}), bf16[8,400,800]{2,1,0:T(8,128)(2,1)}) %all-gather.10.cloned.1.call-update) | async-done | bytes 5120016 | tf_op jit(solution)/shard_map/all_gather | solution.py:615
  182.0 3.3 fusion.22
  185.7 4.9 shard_map.189
  191.8 5.2 shard_map.190.lhs_ref.rhs_ref
  197.0 35.2 %shard_map.191 = f32[128,1600]{1,0:T(8,128)S(1)} custom-call(bf16[1024,800]{1,0:T(8,128)(2,1)S(1)} %shard_map.190.lhs_ref.rhs_ref, bf16[1600,800]{1,0:T(8,128)(2,1)S(1)} %bitcast.94), custom_call_target="tpu_custom_call" | custom-call | flops 2621440000 | bytes 62914560 | tf_op jit(solution)/shard_map/pallas_call | solution.py:229
  232.3 4.4 weight_grad.6
  239.9 21.6 %shard_map.192.lhs_ref = bf16[1024,1600]{1,0:T(8,128)(2,1)S(1)} custom-call(bf16[128,1600]{1,0:T(8,128)(2,1)S(1)} %get-tuple-element.116.refs_0_), custom_call_target="tpu_custom_call" | custom-call | bytes 31457280 | tf_op jit(solution)/shard_map/pallas_call | solution.py:99
  261.5 3.0 weight_grad.5
  264.6 2.7 convolution_convert_fusion.1.g_ref
  267.3 11.7 %attend_back.1.lhs_ref.rhs_ref = bf16[1024,768]{1,0:T(8,128)(2,1)S(1)} custom-call(bf16[1024,768]{1,0:T(8,128)(2,1)S(1)} %convolution_convert_fusion.q_ref.k_ref.v_ref, bf16[1024,768]{1,0:T(8,128)(2,1)S(1)} %convolution_convert_fusion.q_ref.k_ref.v_ref, bf16[1024,768]{1,0:T(8,128)(2,1)S(1)} %convolution_convert_fusion.q_ref.k_ref.v_ref, ...), custom_call_target="tpu_custom_call" | custom-call | flops 2684354560 | bytes 83886080 | tf_op jit(solution)/shard_map/attend_back/pallas_call | solution.py:391
  279.0 4.2 weight_grad.4
  285.4 33.8 %shard_map.194 = f32[128,1600]{1,0:T(8,128)S(1)} custom-call(bf16[1024,768]{1,0:T(8,128)(2,1)S(1)} %attend_back.1.lhs_ref.rhs_ref, bf16[1600,768]{1,0:T(8,128)(2,1)S(1)} %copy-done.15), custom_call_target="tpu_custom_call" | custom-call | flops 2516582400 | bytes 62914560 | tf_op jit(solution)/shard_map/pallas_call | solution.py:229
  321.3 11.0 %sum_everywhere.1 = f32[8,128]{1,0:T(8,128)S(1)} custom-call(f32[16,8,128]{2,1,0:T(8,128)S(1)} %pad.8.tiles_ref), custom_call_target="tpu_custom_call" | custom-call | bytes 15728640 | tf_op jit(solution)/shard_map/sum_everywhere/pallas_call | solution.py:148
  332.3 2.2 convert_element_type.178
  344.5 4.4 weight_grad.7
  351.8 31.7 %collective-permute-done.5 = f16[416,256]{1,0:T(8,128)(2,1)S(1)} collective-permute-done((f16[416,256]{1,0:T(8,128)(2,1)S(1)}, f16[416,256]{1,0:T(8,128)(2,1)S(1)}, u32[]{:S(2)}, u32[]{:S(2)}) %collective-permute-start.5) | collective-permute-done | bytes 213024 | tf_op jit(solution)/shard_map/ppermute | solution.py:466
  383.5 35.4 %shard_map.193 = f32[128,1600]{1,0:T(8,128)S(1)} custom-call(bf16[1024,800]{1,0:T(8,128)(2,1)S(1)} %copy-done.37, bf16[1600,800]{1,0:T(8,128)(2,1)S(1)} %bitcast.91), custom_call_target="tpu_custom_call" | custom-call | flops 2621440000 | bytes 62914560 | tf_op jit(solution)/shard_map/pallas_call | solution.py:229
  421.1 3.0 collective-permute-start.2
  425.3 1.8 collective-permute-start.1
  429.2 3.4 all-to-all-start
  439.9 3.1 multiply_add_fusion.1
  443.0 2.6 reshape.186
  446.3 4.4 all-to-all-start.1
  452.4 60.7 %collective-permute-done.11 = f16[416,800]{1,0:T(8,128)(2,1)} collective-permute-done((f16[416,800]{1,0:T(8,128)(2,1)}, f16[416,800]{1,0:T(8,128)(2,1)}, u32[]{:S(2)}, u32[]{:S(2)}) %collective-permute-start.11) | collective-permute-done | bytes 665632 | tf_op jit(solution)/shard_map/ppermute | solution.py:466
  515.8 28.5 %collective-permute-done.10 = f16[416,800]{1,0:T(8,128)(2,1)} collective-permute-done((f16[416,800]{1,0:T(8,128)(2,1)}, f16[416,800]{1,0:T(8,128)(2,1)}, u32[]{:S(2)}, u32[]{:S(2)}) %collective-permute-start.10) | collective-permute-done | bytes 665632 | tf_op jit(solution)/shard_map/ppermute | solution.py:466
  548.1 2.1 multiply_add_fusion
  551.4 3.6 all-to-all-start.2
  555.0 2.6 all_gather.24
  558.9 2.4 all-gather.1
  562.3 2.0 slice_bitcast_fusion
  564.4 1.9 concatenate.8
  572.1 1.8 add_convert_fusion
  574.1 13.4 %shard_map.195 = f32[100,4800]{1,0:T(8,128)S(1)} custom-call(bf16[4,112,768]{2,1,0:T(8,128)(2,1)S(1)} %pad.9.src_ref), custom_call_target="tpu_custom_call" | custom-call | bytes 20971520 | tf_op jit(solution)/shard_map/pallas_call | solution.py:565
  588.8 2.8 copy.72
  591.7 2.9 reshape.187
  596.0 2.9 reshape.189
  598.9 2.6 copy.75
  601.5 3.1 copy.81
  (203 shorter events, 63.8 us)
Async XLA Ops:
  7.2 3.9 copy-start
  7.2 68.2 %all-gather.6.cloned.1.call-start = ((), (), s32[]{:S(2)}) async-start(), calls=%async_computation.3 | async-start | bytes 4096000 | tf_op jit(solution)/shard_map/all_gather | solution.py:610
  11.0 171.0 %all-gather.10.cloned.1.call-start = ((), (), s32[]{:S(2)}) async-start(), calls=%async_computation.5 | async-start | bytes 7168000 | tf_op jit(solution)/shard_map/all_gather | solution.py:615
  14.2 584.7 %all-gather.8.cloned.1.call-start = ((), (), s32[]{:S(2)}) async-start(), calls=%async_computation.4 | async-start | bytes 2555904 | tf_op jit(solution)/shard_map/all_gather | solution.py:651
  14.3 2.1 copy-start.49
  76.6 5.8 copy-start.16
  89.7 34.6 %copy-start.3 = (bf16[1,128,1600]{2,1,0:T(8,128)(2,1)S(1)}, bf16[1,128,1600]{2,1,0:T(8,128)(2,1)}, u32[]{:S(2)}) copy-start(bf16[1,128,1600]{2,1,0:T(8,128)(2,1)} %copy.63) | copy-start | bytes 1228804
  125.7 21.6 %copy-start.40 = (bf16[1600,1024]{1,0:T(8,128)(2,1)S(1)}, bf16[1600,1024]{1,0:T(8,128)(2,1)}, u32[]{:S(2)}) copy-start(bf16[1600,1024]{1,0:T(8,128)(2,1)} %all-gather.6.cloned.1.call-done) | copy-start | bytes 9830404
  147.4 2.6 copy-start.13
  182.0 3.7 copy-start.14
  185.3 6.5 %copy-start.4 = (bf16[4,1,400,800]{3,2,1,0:T(8,128)(2,1)}, bf16[4,1,400,800]{3,2,1,0:T(8,128)(2,1)S(1)}, u32[]{:S(2)}) copy-start(bf16[4,1,400,800]{3,2,1,0:T(8,128)(2,1)S(1)} %get-tuple-element.120) | copy-start | bytes 7680004
  185.7 6.1 copy-start.10
  232.3 5.6 copy-start.39
  237.8 1.8 copy-start.19
  237.8 2.1 copy-start.21
  264.5 2.7 copy-start.30
  264.6 2.7 copy-start.32
  264.6 2.7 copy-start.34
  267.3 11.7 %copy-start.12 = (bf16[1024,1600]{1,0:T(8,128)(2,1)S(1)}, bf16[1024,1600]{1,0:T(8,128)(2,1)}, u32[]{:S(2)}) copy-start(bf16[1024,1600]{1,0:T(8,128)(2,1)} %fusion.5.lhs_ref) | copy-start | bytes 9830404
  279.0 6.3 %copy-start.15 = (bf16[1600,768]{1,0:T(8,128)(2,1)S(1)}, bf16[1600,768]{1,0:T(8,128)(2,1)}, u32[]{:S(2)}) copy-start(bf16[1600,768]{1,0:T(8,128)(2,1)} %slice.197.rhs_ref) | copy-start | bytes 7372804
  335.5 2.3 copy-start.31
  335.5 3.0 copy-start.22
  336.4 8.1 %copy-start.37 = (bf16[1024,800]{1,0:T(8,128)(2,1)S(1)}, bf16[1024,800]{1,0:T(8,128)(2,1)}, u32[]{:S(2)}) copy-start(bf16[1024,800]{1,0:T(8,128)(2,1)} %copy-done.36) | copy-start | bytes 4915204
  336.4 47.1 %collective-permute-start.5 = (f16[416,256]{1,0:T(8,128)(2,1)S(1)}, f16[416,256]{1,0:T(8,128)(2,1)S(1)}, u32[]{:S(2)}, u32[]{:S(2)}) collective-permute-start(f16[416,256]{1,0:T(8,128)(2,1)S(1)} %convert_element_type.188), channel_id=1, source_target_pairs={{0,16},{8,24},{16,0},{24,8},{1,17},{9,25},{17,1},{25,9},{2,18},{10... | collective-permute-start | bytes 638984 | tf_op jit(solution)/shard_map/ppermute | solution.py:466
  337.8 2.6 copy-start.20
  337.8 83.2 %collective-permute-start.4 = (f16[416,256]{1,0:T(8,128)(2,1)S(1)}, f16[416,256]{1,0:T(8,128)(2,1)S(1)}, u32[]{:S(2)}, u32[]{:S(2)}) collective-permute-start(f16[416,256]{1,0:T(8,128)(2,1)S(1)} %convert_element_type.185), channel_id=1, source_target_pairs={{0,24},{8,0},{16,8},{24,16},{1,25},{9,1},{17,9},{25,17},{2,26},{10... | collective-permute-start | bytes 638984 | tf_op jit(solution)/shard_map/ppermute | solution.py:466
  338.5 4.0 copy-start.18
  339.5 93.1 %collective-permute-start.8 = (f16[416,800]{1,0:T(8,128)(2,1)}, f16[416,800]{1,0:T(8,128)(2,1)}, u32[]{:S(2)}, u32[]{:S(2)}) collective-permute-start(f16[416,800]{1,0:T(8,128)(2,1)} %convert_element_type.200), channel_id=1, source_target_pairs={{0,16},{8,24},{16,0},{24,8},{1,17},{9,25},{17,1},{25,9},{2,18},{10... | collective-permute-start | bytes 1996808 | tf_op jit(solution)/shard_map/ppermute | solution.py:466
  340.4 4.0 copy-start.11
  341.4 93.2 %collective-permute-start.7 = (f16[416,800]{1,0:T(8,128)(2,1)}, f16[416,800]{1,0:T(8,128)(2,1)}, u32[]{:S(2)}, u32[]{:S(2)}) collective-permute-start(f16[416,800]{1,0:T(8,128)(2,1)} %convert_element_type.197), channel_id=1, source_target_pairs={{0,24},{8,0},{16,8},{24,16},{1,25},{9,1},{17,9},{25,17},{2,26},{10... | collective-permute-start | bytes 1996808 | tf_op jit(solution)/shard_map/ppermute | solution.py:466
  343.5 94.0 %collective-permute-start.6 = (f16[416,800]{1,0:T(8,128)(2,1)}, f16[416,800]{1,0:T(8,128)(2,1)}, u32[]{:S(2)}, u32[]{:S(2)}) collective-permute-start(f16[416,800]{1,0:T(8,128)(2,1)} %convert_element_type.194), channel_id=1, source_target_pairs={{0,8},{8,16},{16,24},{24,0},{1,9},{9,17},{17,25},{25,1},{2,10},{10... | collective-permute-start | bytes 1996808 | tf_op jit(solution)/shard_map/ppermute | solution.py:466
  349.9 33.6 %copy-start.5 = (bf16[4,1,400,800]{3,2,1,0:T(8,128)(2,1)S(1)}, bf16[4,1,400,800]{3,2,1,0:T(8,128)(2,1)}, u32[]{:S(2)}) copy-start(bf16[4,1,400,800]{3,2,1,0:T(8,128)(2,1)} %copy-done.4) | copy-start | bytes 7680004
  351.8 76.5 %copy-start.35 = (f32[400,256]{1,0:T(8,128)S(1)}, f32[400,256]{1,0:T(8,128)}, u32[]{:S(2)}) copy-start(f32[400,256]{1,0:T(8,128)} %copy-done.34) | copy-start | bytes 1228804
  383.5 41.8 %collective-permute-start.3 = (f16[416,256]{1,0:T(8,128)(2,1)S(1)}, f16[416,256]{1,0:T(8,128)(2,1)S(1)}, u32[]{:S(2)}, u32[]{:S(2)}) collective-permute-start(f16[416,256]{1,0:T(8,128)(2,1)S(1)} %convert_element_type.182), channel_id=1, source_target_pairs={{0,8},{8,16},{16,24},{24,0},{1,9},{9,17},{17,25},{25,1},{2,10},{10... | collective-permute-start | bytes 638984 | tf_op jit(solution)/shard_map/ppermute | solution.py:466
  419.8 20.1 %copy-start.24 = (f32[400,800]{1,0:T(8,128)S(1)}, f32[400,800]{1,0:T(8,128)}, u32[]{:S(2)}) copy-start(f32[400,800]{1,0:T(8,128)} %copy-done.23) | copy-start | bytes 3840004
  421.1 145.2 %collective-permute-start.2 = (f16[416,768]{1,0:T(8,128)(2,1)}, f16[416,768]{1,0:T(8,128)(2,1)}, u32[]{:S(2)}, u32[]{:S(2)}) collective-permute-start(f16[416,768]{1,0:T(8,128)(2,1)} %convert_element_type.178), channel_id=1, source_target_pairs={{0,16},{8,24},{16,0},{24,8},{1,17},{9,25},{17,1},{25,9},{2,18},{10... | collective-permute-start | bytes 1916936 | tf_op jit(solution)/shard_map/ppermute | solution.py:466
  425.3 142.9 %collective-permute-start.1 = (f16[416,768]{1,0:T(8,128)(2,1)}, f16[416,768]{1,0:T(8,128)(2,1)}, u32[]{:S(2)}, u32[]{:S(2)}) collective-permute-start(f16[416,768]{1,0:T(8,128)(2,1)} %convert_element_type.175), channel_id=1, source_target_pairs={{0,24},{8,0},{16,8},{24,16},{1,25},{9,1},{17,9},{25,17},{2,26},{10... | collective-permute-start | bytes 1916936 | tf_op jit(solution)/shard_map/ppermute | solution.py:466
  429.2 16.4 %all-to-all-start = ((bf16[4,100,256]{2,1,0:T(8,128)(2,1)}), bf16[4,100,256]{2,1,0:T(8,128)(2,1)S(1)}, u32[]{:S(2)}, u32[]{:S(2)}) async-start(bf16[4,100,256]{2,1,0:T(8,128)(2,1)} %reshape.185), calls=%async_computation | async-start | bytes 425984 | tf_op jit(solution)/shard_map/all_to_all | solution.py:654
  432.6 80.5 %collective-permute-start.11 = (f16[416,800]{1,0:T(8,128)(2,1)}, f16[416,800]{1,0:T(8,128)(2,1)}, u32[]{:S(2)}, u32[]{:S(2)}) collective-permute-start(f16[416,800]{1,0:T(8,128)(2,1)} %convert_element_type.209), channel_id=1, source_target_pairs={{0,16},{8,24},{16,0},{24,8},{1,17},{9,25},{17,1},{25,9},{2,18},{10... | collective-permute-start | bytes 1996808 | tf_op jit(solution)/shard_map/ppermute | solution.py:466
  434.6 109.8 %collective-permute-start.10 = (f16[416,800]{1,0:T(8,128)(2,1)}, f16[416,800]{1,0:T(8,128)(2,1)}, u32[]{:S(2)}, u32[]{:S(2)}) collective-permute-start(f16[416,800]{1,0:T(8,128)(2,1)} %convert_element_type.206), channel_id=1, source_target_pairs={{0,24},{8,0},{16,8},{24,16},{1,25},{9,1},{17,9},{25,17},{2,26},{10... | collective-permute-start | bytes 1996808 | tf_op jit(solution)/shard_map/ppermute | solution.py:466
  437.4 108.8 %collective-permute-start.9 = (f16[416,800]{1,0:T(8,128)(2,1)}, f16[416,800]{1,0:T(8,128)(2,1)}, u32[]{:S(2)}, u32[]{:S(2)}) collective-permute-start(f16[416,800]{1,0:T(8,128)(2,1)} %convert_element_type.203), channel_id=1, source_target_pairs={{0,8},{8,16},{16,24},{24,0},{1,9},{9,17},{17,25},{25,1},{2,10},{10... | collective-permute-start | bytes 1996808 | tf_op jit(solution)/shard_map/ppermute | solution.py:466
  445.6 5.1 copy-start.29
  446.3 105.2 %all-to-all-start.1 = ((f32[4,100,800]{2,1,0:T(8,128)}), f32[4,100,800]{2,1,0:T(8,128)}, u32[]{:S(2)}, u32[]{:S(2)}) async-start(f32[4,100,800]{2,1,0:T(8,128)} %reshape.186), calls=%async_computation.1 | async-start | bytes 2981888 | tf_op jit(solution)/shard_map/all_to_all | solution.py:654
  513.1 57.0 %collective-permute-start = (f16[416,768]{1,0:T(8,128)(2,1)}, f16[416,768]{1,0:T(8,128)(2,1)}, u32[]{:S(2)}, u32[]{:S(2)}) collective-permute-start(f16[416,768]{1,0:T(8,128)(2,1)} %convert_element_type.172), channel_id=1, source_target_pairs={{0,8},{8,16},{16,24},{24,0},{1,9},{9,17},{17,25},{25,1},{2,10},{10... | collective-permute-start | bytes 1916936 | tf_op jit(solution)/shard_map/ppermute | solution.py:466
  551.4 43.1 %all-to-all-start.2 = ((f32[4,100,800]{2,1,0:T(8,128)}), f32[4,100,800]{2,1,0:T(8,128)S(1)}, u32[]{:S(2)}, u32[]{:S(2)}) async-start(f32[4,100,800]{2,1,0:T(8,128)} %reshape.188), calls=%async_computation.2 | async-start | bytes 2981888 | tf_op jit(solution)/shard_map/all_to_all | solution.py:654
  555.0 3.9 copy-start.42
  562.3 9.7 %copy-start.27 = (f32[400,768]{1,0:T(8,128)S(1)}, f32[400,768]{1,0:T(8,128)}, u32[]{:S(2)}) copy-start(f32[400,768]{1,0:T(8,128)} %copy-done.26) | copy-start | bytes 3686404
  601.5 3.1 copy-start.1
  (20 other events, 24.2 us)
Sparse Core Ops, SparseCore 0:
  11.2 64.2 all-gather.5
  77.5 104.4 all-gather.9
  321.0 10.4 all-gather.7
